TPU v7x, 512 devices: a whole 4x4x16 slice. The times are simulated.
512 devices in a mesh: seq: 64 (over z_lo, x, core), batch: 8 (over y, z_hi).
Axes of the slice: x: 4, y: 4, z: 16 (z_hi: 2, z_lo: 8; z = z_hi * 8 + z_lo), core: 2. Of those that a mesh axis runs over, the one named last changes fastest.
Arguments:
- activ: bfloat16 [8, 8192, 384], P('batch', 'seq'), may hold values from -6 to 6
- gain: float32 [384], replicated, may hold values from 0.1 to 1.9
- weight: bfloat16 [5, 384, 448], P(None, 'seq'), may hold values from -0.125 to 0.125
- bias: float32 [448], replicated, may hold values from -0.5 to 0.5
- cotangent: bfloat16 [8, 4096, 448], P('batch', 'seq'), may hold values from -6 to 6
Outputs:
- pooled: bfloat16 [8, 4096, 448], P('batch', 'seq')
- grad_input: bfloat16 [8, 8192, 384], P('batch', 'seq')
- grad_weight: float32 [5, 384, 448], P(None, 'seq')
- grad_gain: float32 [384], replicated
- grad_bias: float32 [448], replicated
All inputs are finite; a program needn't handle non-finite values.
Results may differ from a plain program's by a relative error of at most 0.0043.
Values may be sent and summed in bfloat16 or wider, within the bound.
A program may use at most 64 MiB of HBM per device.

v0:
```python
import functools

import jax
import jax.numpy as jnp
from jax import lax
from jax.sharding import Mesh
from jax.sharding import PartitionSpec as P

SEQ = ("seq_0", "seq_1", "seq_2")
BATCH = ("batch_0", "batch_1")
SEQ_BATCH = ("seq_0", "seq_1", "seq_2", "batch_0", "batch_1")


def padded(value, sides, width):
    for axis, dim in sides:
        size, length = (lax.axis_size(axis), value.shape[dim])
        up = [(i, (i + 1) % size) for i in range(size - 1)]
        down = [(j, i) for i, j in up]
        last = lax.slice_in_dim(value, length - width, length, axis=dim)
        first = lax.slice_in_dim(value, 0, width, axis=dim)
        before = lax.ppermute(last, axis, up)
        after = lax.ppermute(first, axis, down)
        value = jnp.concatenate([before, value, after], axis=dim)
    return value


def from_everyone(value, axis):
    size = lax.axis_size(axis)
    return lax.all_to_all(
        jnp.broadcast_to(value[None], (size, *value.shape)), axis, 0, 0, tiled=True
    )


def in_order(blocks, dim):
    blocks = jnp.moveaxis(blocks, 0, dim)
    dims = blocks.shape
    return blocks.reshape(*dims[:dim], dims[dim] * dims[dim + 1], *dims[dim + 2 :])


def gather_axes(value, axes, dim):
    far, near = axes
    first = from_everyone(value, far)
    blocks = jnp.swapaxes(from_everyone(first, near), 0, 1)
    return in_order(blocks.reshape(-1, *value.shape), dim)


def in_blocks(value, dim, size):
    before, after = (value.shape[:dim], value.shape[dim + 1 :])
    return jnp.moveaxis(value.reshape(*before, size, -1, *after), dim, 0)


def summed_on_arrival(value, axis, dim):
    blocks = in_blocks(value, dim, lax.axis_size(axis))
    arrived = lax.all_to_all(blocks, axis, split_axis=0, concat_axis=0, tiled=True)
    return arrived.sum(axis=0)


def sum_in_two_steps(value, axes, dim):
    far, near = axes
    own = summed_on_arrival(in_blocks(value, dim, lax.axis_size(far)), near, dim + 1)
    return jnp.sum(lax.all_to_all(own, far, 0, 0, tiled=True), axis=0)


def over_copies(value, axis):
    return from_everyone(value, axis).sum(axis=0)


def over_axes(value, axes):
    return functools.reduce(lax.psum, axes, value)


def per_device(activ, gain, weight, bias, cotangent):
    row_count = activ.shape[1]
    seq_count = activ.shape[0]
    out_width = weight.shape[2]
    taps = weight.shape[0]
    scaled = activ.astype(jnp.float32) * gain
    activated, gelu_back = jax.vjp(jax.nn.gelu, scaled)
    widened = padded(activated.astype(jnp.bfloat16), ((SEQ, 1),), 2)
    cot_wide = padded(cotangent, ((SEQ, 1),), 1)
    grad_wide = (0.5 * jnp.repeat(cot_wide.astype(jnp.float32), 2, axis=1)).astype(jnp.bfloat16)
    grad_local = grad_wide[:, 2 : 2 + row_count]
    conv_zero = jnp.zeros((seq_count, row_count, out_width), jnp.float32)
    shard_piece = gather_axes(weight, (("seq_0", "seq_1"), "seq_2"), 1)
    conv_part = conv_zero
    running = conv_part
    columns = widened
    for offset in range(shard_piece.shape[0]):
        running = running + jnp.einsum(
            "btc,cd->btd",
            columns[:, offset : offset + row_count],
            shard_piece[offset],
            preferred_element_type=jnp.float32,
        )
    conv_part = running
    result = jnp.zeros((seq_count, row_count, shard_piece.shape[1]), jnp.float32)
    for offset in range(shard_piece.shape[0]):
        result = result + jnp.einsum(
            "btd,cd->btc",
            grad_wide[:, 4 - offset : 4 - offset + row_count],
            shard_piece[offset],
            preferred_element_type=jnp.float32,
        )
    conv_out = conv_part
    conv_out = conv_out + bias
    pooled = (0.5 * (conv_out[:, 0::2] + conv_out[:, 1::2])).astype(jnp.bfloat16)
    grad_pre = gelu_back(result)[0]
    grad_input = (grad_pre * gain).astype(jnp.bfloat16)
    columns = widened
    own_rows = sum_in_two_steps(
        jnp.stack(
            [
                jnp.einsum(
                    "btc,btd->cd",
                    columns[:, offset : offset + row_count],
                    grad_local,
                    preferred_element_type=jnp.float32,
                )
                for offset in range(taps)
            ],
            axis=1,
        ),
        (("seq_0", "seq_1"), "seq_2"),
        0,
    )
    weight_total = over_copies(jnp.transpose(own_rows, (1, 0, 2)), BATCH)
    gain_local = jnp.sum(grad_pre * activ.astype(jnp.float32), axis=(0, 1))
    bias_local = jnp.sum(cotangent.astype(jnp.float32), axis=(0, 1))
    gain_total, bias_total = (over_axes(gain_local, SEQ_BATCH), over_axes(bias_local, SEQ_BATCH))
    factor = float(lax.axis_size(SEQ) * lax.axis_size(BATCH) * row_count * seq_count) ** (-0.5)
    return (pooled, grad_input, weight_total * factor, gain_total * factor, bias_total * factor)


def solution(mesh):
    finer = Mesh(
        mesh.devices.reshape(8, 4, 2, 4, 2), ("seq_0", "seq_1", "seq_2", "batch_0", "batch_1")
    )
    in_specs = (P(BATCH, SEQ, None), P(), P(None, SEQ, None), P(), P(BATCH, SEQ, None))
    out_specs = (P(BATCH, SEQ, None), P(BATCH, SEQ, None), P(None, SEQ, None), P(), P())
    return jax.shard_map(
        per_device, mesh=finer, in_specs=in_specs, out_specs=out_specs, check_vma=False
    )
```

profile of v0, /device:TPU:32, one launch (start us, length us, event | category | flops | bytes accessed | tf_op | source)
XLA Modules:
  0.0 351.5 jit_solution(10011389640740428137)
XLA Ops:
  0.6 2.0 broadcast_in_dim.8
  2.6 15.2 %all-to-all-start = ((bf16[32,5,6,448]{3,2,1,0:T(8,128)(2,1)}), bf16[32,5,6,448]{3,2,1,0:T(8,128)(2,1)S(1)}, u32[]{:S(2)}, u32[]{:S(2)}) async-start(bf16[32,5,6,448]{3,2,1,0:T(8,128)(2,1)} %broadcast_in_dim.8), calls=%async_computation | async-start | bytes 2621440 | tf_op jit(solution)/shard_map/all_to_all | solution.py:29
  17.9 3.5 collective-permute-start.3
  23.3 20.7 %collective-permute-done.2 = bf16[1,1,448]{2,1,0:T(2,128)(2,1)S(1)} collective-permute-done((bf16[1,1,448]{2,1,0:T(2,128)(2,1)S(1)}, bf16[1,1,448]{2,1,0:T(2,128)(2,1)S(1)}, u32[]{:S(2)}, u32[]{:S(2)}) %collective-permute-start.2) | collective-permute-done | bytes 928 | tf_op jit(solution)/shard_map/ppermute | solution.py:21
  44.2 35.6 %all-to-all-done = bf16[32,5,6,448]{3,2,1,0:T(8,128)(2,1)S(1)} async-done(((bf16[32,5,6,448]{3,2,1,0:T(8,128)(2,1)}), bf16[32,5,6,448]{3,2,1,0:T(8,128)(2,1)S(1)}, u32[]{:S(2)}, u32[]{:S(2)}) %all-to-all-start) | async-done | bytes 860192 | tf_op jit(solution)/shard_map/all_to_all | solution.py:29
  80.4 5.3 %all_to_all.25 = bf16[2,32,5,6,448]{4,1,3,2,0:T(8,128)(2,1)S(1)} all-to-all(bf16[2,32,5,6,448]{4,1,3,2,0:T(8,128)(2,1)S(1)} %broadcast_in_dim.9), channel_id=1, replica_groups=mesh['seq_0'=8,'seq_1'=4,'seq_2'=2,'batch_0'=4,'batch_1'=2] {'seq_2'}, dimensions={0} | all-to-all | bytes 3440640 | tf_op jit(solution)/shard_map/all_to_all | solution.py:29
  85.7 3.3 copy.104
  89.0 4.4 %reshape.168 = bf16[64,5,6,448]{3,0,2,1:T(8,128)(2,1)S(1)} reshape(bf16[32,2,5,6,448]{4,1,0,3,2:T(2,128)(2,1)} %copy.104) | data formatting | bytes 3440640 | tf_op jit(solution)/shard_map/reshape | solution.py:44
  102.4 2.0 collective-permute-start
  104.4 5.6 %collective-permute-start.1 = (bf16[1,2,384]{2,1,0:T(2,128)(2,1)S(1)}, bf16[1,2,384]{2,1,0:T(2,128)(2,1)S(1)}, u32[]{:S(2)}, u32[]{:S(2)}) collective-permute-start(bf16[1,2,384]{2,1,0:T(2,128)(2,1)S(1)} %get-tuple-element.59), channel_id=1, source_target_pairs={{8,0},{16,8},{24,16},{32,24},{40,32},{48,40},{56,48},{64,56},{72,6... | collective-permute-start | bytes 4616 | tf_op jit(solution)/shard_map/ppermute | solution.py:22
  117.9 2.5 copy.121
  120.5 7.9 %all_to_all.26 = f32[2,32,6,5,448]{4,1,2,3,0:T(8,128)} all-to-all(f32[2,32,6,5,448]{4,1,2,3,0:T(8,128)S(1)} %copy.121), channel_id=1, replica_groups=mesh['seq_0'=8,'seq_1'=4,'seq_2'=2,'batch_0'=4,'batch_1'=2] {'seq_2'}, dimensions={0} | all-to-all | bytes 6881280 | tf_op jit(solution)/shard_map/all_to_all | solution.py:54
  128.4 2.9 reduce_sum.45
  131.3 2.7 copy.123
  134.0 8.0 %all-to-all-start.3 = ((f32[32,6,5,448]{3,1,2,0:T(8,128)}), f32[32,6,5,448]{3,1,2,0:T(8,128)S(1)}, u32[]{:S(2)}, u32[]{:S(2)}) async-start(f32[32,6,5,448]{3,1,2,0:T(8,128)} %copy.123), calls=%async_computation.3 | async-start | bytes 5242880 | tf_op jit(solution)/shard_map/all_to_all | solution.py:61
  142.0 123.9 %all-reduce = (f32[384]{0:T(512)S(1)}, f32[448]{0:T(512)S(1)}) all-reduce(f32[384]{0:T(512)S(1)} %get-tuple-element.50, f32[448]{0:T(512)S(1)} %convert_reduce_fusion), channel_id=1, replica_groups=mesh['seq_0'=8,'seq_1'=4,'seq_2'=2,'batch_0'=4,'batch_1'=2] {'seq_0'}, use_global_device_ids=true, to_apply=%region_4.0 | all-reduce | flops 832 | bytes 6656 | tf_op jit(solution)/shard_map/psum | solution.py:69
  265.9 9.9 %all-reduce.2 = (f32[384]{0:T(512)S(1)}, f32[448]{0:T(512)S(1)}) all-reduce(f32[384]{0:T(512)S(1)} %get-tuple-element.35, f32[448]{0:T(512)S(1)} %get-tuple-element.36), channel_id=1, replica_groups=mesh['seq_0'=8,'seq_1'=4,'seq_2'=2,'batch_0'=4,'batch_1'=2] {'seq_1'}, use_global_device_ids=true, to_apply=%region_5.0 | all-reduce | flops 832 | bytes 6656 | tf_op jit(solution)/shard_map/psum | solution.py:69
  275.8 2.5 all-reduce.4
  278.3 10.7 %all-reduce.1 = (f32[384]{0:T(512)S(1)}, f32[448]{0:T(512)S(1)}) all-reduce(f32[384]{0:T(512)S(1)} %get-tuple-element.43, f32[448]{0:T(512)S(1)} %get-tuple-element.44), channel_id=1, replica_groups=mesh['seq_0'=8,'seq_1'=4,'seq_2'=2,'batch_0'=4,'batch_1'=2] {'batch_0'}, use_global_device_ids=true, to_apply=%region_7.0 | all-reduce | flops 832 | bytes 6656 | tf_op jit(solution)/shard_map/psum | solution.py:69
  289.0 13.6 %all-reduce.3 = (f32[384]{0:T(512)S(1)}, f32[448]{0:T(512)S(1)}) all-reduce(f32[384]{0:T(512)S(1)} %get-tuple-element.37, f32[448]{0:T(512)S(1)} %get-tuple-element.38), channel_id=1, replica_groups=mesh['seq_0'=8,'seq_1'=4,'seq_2'=2,'batch_0'=4,'batch_1'=2] {'batch_1'}, use_global_device_ids=true, to_apply=%region_8.0 | all-reduce | flops 832 | bytes 6656 | tf_op jit(solution)/shard_map/psum | solution.py:69
  304.4 7.9 %all-to-all-start.4 = ((f32[8,5,6,448]{3,2,1,0:T(8,128)}), f32[8,5,6,448]{3,2,1,0:T(8,128)S(1)}, u32[]{:S(2)}, u32[]{:S(2)}) async-start(f32[8,5,6,448]{3,2,1,0:T(8,128)} %broadcast_in_dim.11), calls=%async_computation.4 | async-start | bytes 1310720 | tf_op jit(solution)/shard_map/all_to_all | solution.py:29
  318.4 3.9 %slice.90 = f32[1,64,448]{1,2,0:T(8,128)S(1)} slice(f32[1,128,448]{1,2,0:T(8,128)S(1)} %fusion.6), slice={[0:1:1], [0:128:2], [0:448:1]} | slice | bytes 229376 | tf_op jit(solution)/shard_map/slice | solution.py:106
  322.4 4.0 %slice.91 = f32[1,64,448]{1,2,0:T(8,128)S(1)} slice(f32[1,128,448]{1,2,0:T(8,128)S(1)} %fusion.6), slice={[0:1:1], [1:128:2], [0:448:1]} | slice | bytes 229376 | tf_op jit(solution)/shard_map/slice | solution.py:106
  327.2 23.6 %all-to-all-done.4 = f32[8,5,6,448]{3,2,1,0:T(8,128)S(1)} async-done(((f32[8,5,6,448]{3,2,1,0:T(8,128)}), f32[8,5,6,448]{3,2,1,0:T(8,128)S(1)}, u32[]{:S(2)}, u32[]{:S(2)}) %all-to-all-start.4) | async-done | bytes 430112 | tf_op jit(solution)/shard_map/all_to_all | solution.py:29
  (74 shorter events, 28.7 us)
Async XLA Ops:
  0.6 17.2 %copy-start.4 = (bf16[1,64,448]{2,1,0:T(8,128)(2,1)S(1)}, bf16[1,64,448]{2,1,0:T(8,128)(2,1)}, u32[]{:S(2)}) copy-start(bf16[1,64,448]{2,1,0:T(8,128)(2,1)} %param.9) | copy-start | bytes 172036
  2.6 77.2 %all-to-all-start = ((bf16[32,5,6,448]{3,2,1,0:T(8,128)(2,1)}), bf16[32,5,6,448]{3,2,1,0:T(8,128)(2,1)S(1)}, u32[]{:S(2)}, u32[]{:S(2)}) async-start(bf16[32,5,6,448]{3,2,1,0:T(8,128)(2,1)} %broadcast_in_dim.8), calls=%async_computation | async-start | bytes 2621440 | tf_op jit(solution)/shard_map/all_to_all | solution.py:29
  17.9 5.4 %collective-permute-start.3 = (bf16[1,1,448]{2,1,0:T(2,128)(2,1)S(1)}, bf16[1,1,448]{2,1,0:T(2,128)(2,1)S(1)}, u32[]{:S(2)}, u32[]{:S(2)}) collective-permute-start(bf16[1,1,448]{2,1,0:T(2,128)(2,1)S(1)} %get-tuple-element.62), channel_id=1, source_target_pairs={{8,0},{16,8},{24,16},{32,24},{40,32},{48,40},{56,48},{64,56},{72,6... | collective-permute-start | bytes 2696 | tf_op jit(solution)/shard_map/ppermute | solution.py:22
  21.3 22.7 %collective-permute-start.2 = (bf16[1,1,448]{2,1,0:T(2,128)(2,1)S(1)}, bf16[1,1,448]{2,1,0:T(2,128)(2,1)S(1)}, u32[]{:S(2)}, u32[]{:S(2)}) collective-permute-start(bf16[1,1,448]{2,1,0:T(2,128)(2,1)S(1)} %get-tuple-element.61), channel_id=1, source_target_pairs={{0,8},{8,16},{16,24},{24,32},{32,40},{40,48},{48,56},{56,64},{64,7... | collective-permute-start | bytes 2696 | tf_op jit(solution)/shard_map/ppermute | solution.py:21
  96.4 4.7 %copy-start.2 = (bf16[384,448]{1,0:T(8,128)(2,1)}, bf16[384,448]{1,0:T(8,128)(2,1)S(1)}, u32[]{:S(2)}) copy-start(bf16[384,448]{1,0:T(8,128)(2,1)S(1)} %squeeze.20) | copy-start | bytes 1032196
  97.8 3.6 %copy-start.6 = (bf16[1,128,384]{2,1,0:T(8,128)(2,1)S(1)}, bf16[1,128,384]{2,1,0:T(8,128)(2,1)}, u32[]{:S(2)}) copy-start(bf16[1,128,384]{2,1,0:T(8,128)(2,1)} %param.5) | copy-start | bytes 294916
  97.8 3.6 %copy-start.7 = (f32[384]{0:T(512)S(1)}, f32[384]{0:T(512)}, u32[]{:S(2)}) copy-start(f32[384]{0:T(512)} %param.6) | copy-start | bytes 4612
  98.0 4.3 %copy-start = (bf16[384,448]{1,0:T(8,128)(2,1)}, bf16[384,448]{1,0:T(8,128)(2,1)S(1)}, u32[]{:S(2)}) copy-start(bf16[384,448]{1,0:T(8,128)(2,1)S(1)} %squeeze.22) | copy-start | bytes 1032196
  99.7 11.8 %copy-start.1 = (bf16[384,448]{1,0:T(8,128)(2,1)}, bf16[384,448]{1,0:T(8,128)(2,1)S(1)}, u32[]{:S(2)}) copy-start(bf16[384,448]{1,0:T(8,128)(2,1)S(1)} %squeeze.23) | copy-start | bytes 1032196
  100.1 12.8 %copy-start.3 = (bf16[384,448]{1,0:T(8,128)(2,1)}, bf16[384,448]{1,0:T(8,128)(2,1)S(1)}, u32[]{:S(2)}) copy-start(bf16[384,448]{1,0:T(8,128)(2,1)S(1)} %squeeze.24) | copy-start | bytes 1032196
  102.4 7.9 %collective-permute-start = (bf16[1,2,384]{2,1,0:T(2,128)(2,1)S(1)}, bf16[1,2,384]{2,1,0:T(2,128)(2,1)S(1)}, u32[]{:S(2)}, u32[]{:S(2)}) collective-permute-start(bf16[1,2,384]{2,1,0:T(2,128)(2,1)S(1)} %get-tuple-element.60), channel_id=1, source_target_pairs={{0,8},{8,16},{16,24},{24,32},{32,40},{40,48},{48,56},{56,64},{64,7... | collective-permute-start | bytes 4616 | tf_op jit(solution)/shard_map/ppermute | solution.py:21
  104.4 6.9 %collective-permute-start.1 = (bf16[1,2,384]{2,1,0:T(2,128)(2,1)S(1)}, bf16[1,2,384]{2,1,0:T(2,128)(2,1)S(1)}, u32[]{:S(2)}, u32[]{:S(2)}) collective-permute-start(bf16[1,2,384]{2,1,0:T(2,128)(2,1)S(1)} %get-tuple-element.59), channel_id=1, source_target_pairs={{8,0},{16,8},{24,16},{32,24},{40,32},{48,40},{56,48},{64,56},{72,6... | collective-permute-start | bytes 4616 | tf_op jit(solution)/shard_map/ppermute | solution.py:22
  134.0 169.2 %all-to-all-start.3 = ((f32[32,6,5,448]{3,1,2,0:T(8,128)}), f32[32,6,5,448]{3,1,2,0:T(8,128)S(1)}, u32[]{:S(2)}, u32[]{:S(2)}) async-start(f32[32,6,5,448]{3,1,2,0:T(8,128)} %copy.123), calls=%async_computation.3 | async-start | bytes 5242880 | tf_op jit(solution)/shard_map/all_to_all | solution.py:61
  303.2 13.9 %copy-start.5 = (f32[448]{0:T(512)S(1)}, f32[448]{0:T(512)}, u32[]{:S(2)}) copy-start(f32[448]{0:T(512)} %param.8) | copy-start | bytes 5380
  304.4 46.4 %all-to-all-start.4 = ((f32[8,5,6,448]{3,2,1,0:T(8,128)}), f32[8,5,6,448]{3,2,1,0:T(8,128)S(1)}, u32[]{:S(2)}, u32[]{:S(2)}) async-start(f32[8,5,6,448]{3,2,1,0:T(8,128)} %broadcast_in_dim.11), calls=%async_computation.4 | async-start | bytes 1310720 | tf_op jit(solution)/shard_map/all_to_all | solution.py:29
where the time goes:
time: 353 us; the launch traced here: 352 us
  blocking collectives  174 us (49%)
  waiting for transfers between devices  81 us (23%)
  starting transfers between devices  44.2 us (13%)
  local copies, waits for them, and re-layouts  32.7 us (9%)
  matrix products  13.4 us (4%)
  other arithmetic  5.28 us (1%)
    psum x5, blocking collectives, over_axes(): return functools.reduce(lax.psum, axes, value)  161 us
    all_to_all x2, waiting for transfers between devices, from_everyone(): lax.all_to_all(jnp.broadcast_to(value[None], (size, *value.shape)), axis,...  59.2 us
    all_to_all x2, starting transfers between devices, from_everyone(): lax.all_to_all(jnp.broadcast_to(value[None], (size, *value.shape)), axis,...  23.1 us
    ppermute x2, waiting for transfers between devices, padded(): before = lax.ppermute(last, axis, up)  20.7 us
    ppermute x2, starting transfers between devices, padded(): after = lax.ppermute(first, axis, down)  9.08 us
    all_to_all x1, starting transfers between devices, sum_in_two_steps(): return jnp.sum(lax.all_to_all(own, far, 0, 0, tiled=True), axis=0)  7.97 us
    all_to_all x1, blocking collectives, summed_on_arrival(): lax.all_to_all(blocks, axis, split_axis=0, concat_axis=0, tiled=True)  7.92 us
  transfers between devices with their start and end apart: 7, of which 4 were waited for; matrix products, arithmetic and copies ran while one was open for 4% of the time, Pallas kernels for 0%

commit v1 on v0

v1 whole, which is shorter than its diff:
```python
import dataclasses
import functools

import jax
import jax.numpy as jnp
from jax import lax
from jax.experimental import pallas as pl
from jax.experimental.pallas import tpu as pltpu
from jax.sharding import PartitionSpec as P

MESH = pl.DeviceIdType.MESH
F32 = jnp.float32
BF16 = jnp.bfloat16
HI = lax.Precision.HIGHEST
ROOT = 0.7978845608028654
CUBE = 0.044715
PAD = 8


@dataclasses.dataclass(frozen=True)
class Plan:
    nx: int = 4
    ny: int = 4
    nzl: int = 8
    nzh: int = 2
    own: int = 6
    taps: int = 5
    rows: int = 128
    cout: int = 448

    @property
    def nz(self):
        return self.nzl * self.nzh

    @property
    def cin(self):
        return self.own * self.nzl * self.nx * 2

    @property
    def block(self):
        return self.own * self.nzl

    @property
    def half(self):
        return self.block * self.nx

    @property
    def halfp(self):
        return -(-self.half // 128) * 128

    @property
    def coutp(self):
        return self.ny * 128

    @property
    def offsets(self):
        far = self.nzl // 2
        return tuple(range(1, far + 1)) + tuple(-o for o in range(1, self.nzl - far))


def dot(a, b, dims, precision=None):
    return lax.dot_general(a, b, (dims, ((), ())), precision=precision, preferred_element_type=F32)


NN = ((1,), (0,))
NT = ((1,), (1,))
TN = ((0,), (0,))


def kernel(
    plan, factor,
    activ, gain, weight, bias, cot,
    pooled, grad_input, grad_weight, grad_gain, grad_bias,
    act_p, cot_p, act_h, cot_h, sel, af, gf, ct, zb, wf, wx, dws, dwo, yr, xs, xo, xr, zo, zs, zr, ya,
    cks, io, gi_s, gi_r, pf_s, pf_r, gx, gt, gy, gs, gz,
    s_loc, r_loc, s_az, r_az, s_ax, r_ax, s_y, r_y, s_x, r_x, s_z, r_z, s_ya, r_ya, s_gx, r_gx, s_gy, r_gy, s_gz, r_gz,
):
    p = plan
    nx, ny, nz, nzl = p.nx, p.ny, p.nz, p.nzl
    rows, half, block, own, taps = p.rows, p.half, p.block, p.own, p.taps
    pairs = rows // 2
    seq, batch = lax.axis_index("seq"), lax.axis_index("batch")
    core = seq % 2
    x = (seq // 2) % nx
    z_lo = seq // (2 * nx)
    z_hi = batch % p.nzh
    y = batch // p.nzh
    z = z_hi * nzl + z_lo
    sign = 1 - 2 * core
    other = 1 - core

    def device(zz, xx, cc, yy):
        return ((zz % nzl) * (2 * nx) + xx * 2 + cc, yy * p.nzh + zz // nzl)

    def at_z(d):
        return (z + d + nz) % nz

    def at_x(d):
        return (x + d) % nx

    def at_y(d):
        return (y + d) % ny

    chip = z * nx + x
    chips = nz * nx
    nxt = (chip + 1) % chips
    prv = (chip + chips - 1) % chips

    partner = device(z, x, other, y)

    def chip_core(c, cc):
        return device(c // nx, c % nx, cc, y)

    barrier = pltpu.get_barrier_semaphore()
    peers = [partner]
    peers += [device(z, at_x(d), cc, y) for d in range(1, nx) for cc in (core, other)]
    peers += [device(z, x, core, at_y(d)) for d in range(1, ny)]
    far = nzl // 2
    peers += [device(at_z(s * o), x, core, y) for o in range(1, far + 1) for s in (1, -1)]
    peers += [chip_core(c, cc) for c in (nxt, prv) for cc in (0, 1)]
    for peer in peers:
        pl.semaphore_signal(barrier, inc=1, device_id=peer, device_id_type=MESH)

    q = lax.broadcasted_iota(jnp.int32, (p.cin, p.halfp), 1)
    r = lax.broadcasted_iota(jnp.int32, (p.cin, p.halfp), 0)
    chan = own * ((q % block) // own * (2 * nx) + (q // block) * 2) + q % own
    valid = q < half
    sel[0] = jnp.where(valid & (r == chan), 1.0, 0.0).astype(BF16)
    sel[1] = jnp.where(valid & (r == chan + own), 1.0, 0.0).astype(BF16)
    mine = sel[core]

    ct[...] = jnp.zeros_like(ct)
    tiles = p.halfp // 128

    def put(start, value):
        for t in range(tiles):
            af[t, pl.ds(start, value.shape[0]), :] = value[:, 128 * t:128 * t + 128]

    put(pl.multiple_of(PAD + rows * core, 8), dot(activ[0], mine, NN))
    ct[pl.ds(pl.multiple_of(PAD + pairs * core, 8), pairs), 0:p.cout] = cot[0].astype(F32)
    gain_half = dot(jnp.broadcast_to(gain[...], (8, p.cin)), mine.astype(F32), NN, HI)[0:1]

    pl.semaphore_wait(barrier, len(peers))

    started = []

    def send(src, dst, s, r_, to):
        copy = pltpu.make_async_remote_copy(
            src_ref=src, dst_ref=dst, send_sem=s, recv_sem=r_, device_id=to, device_id_type=MESH
        )
        copy.start()
        started.append(copy)
        return copy

    c_act = send(activ.at[0], act_p, s_loc.at[0], r_loc.at[0], partner)
    c_cot = send(cot.at[0], cot_p, s_loc.at[1], r_loc.at[1], partner)
    edge = 16
    up_chip = jnp.where(core == 1, nxt, prv)
    side = core
    halos = []
    a_edge = pl.ds(pl.multiple_of(core * (rows - edge), edge), edge)
    c_edge = pl.ds(pl.multiple_of(core * (pairs - edge), edge), edge)
    for i, cc in enumerate((0, 1)):
        to = chip_core(up_chip, cc)
        halos.append(send(activ.at[0, a_edge], act_h.at[side], s_loc.at[2 + i], r_loc.at[2 + side], to))
        halos.append(send(cot.at[0, c_edge], cot_h.at[side], s_loc.at[4 + i], r_loc.at[4 + side], to))
    c_az = []
    for i, o in enumerate(p.offsets):
        to = device(at_z(sign * o), x, core, y)
        c_az.append(send(weight, zb.at[z_lo], s_az.at[i], r_az.at[i], to))
    zb[z_lo] = weight[...]

    c_act.wait_recv()
    put(pl.multiple_of(PAD + rows * other, 8), dot(act_p[...], mine, NN))
    c_cot.wait_recv()
    ct[pl.ds(pl.multiple_of(PAD + pairs * other, 8), pairs), 0:p.cout] = cot_p[...].astype(F32)
    for s in (0, 1):
        for src, dst, i in ((activ.at[0, a_edge], act_h, 2), (cot.at[0, c_edge], cot_h, 4)):
            pltpu.make_async_remote_copy(
                src_ref=src, dst_ref=dst.at[s], send_sem=s_loc.at[i], recv_sem=r_loc.at[i + s],
                device_id=partner, device_id_type=MESH,
            ).wait_recv()
    place = z_lo * nx + x
    before = jnp.where(place > 0, 1.0, 0.0).astype(F32)
    after = jnp.where(place < nzl * nx - 1, 1.0, 0.0).astype(F32)
    put(0, (dot(act_h[1], mine, NN) * before)[edge - PAD:edge])
    put(PAD + 2 * rows, (dot(act_h[0], mine, NN) * after)[0:PAD])
    ct[0:PAD, 0:p.cout] = (cot_h[1].astype(F32) * before)[edge - PAD:edge]
    ct[PAD + rows:, 0:p.cout] = (cot_h[0].astype(F32) * after)[0:PAD]

    for t in range(tiles):
        v = af[t] * gain_half[:, 128 * t:128 * t + 128]
        gf[t] = (0.5 * v * (1.0 + jnp.tanh(ROOT * (v + CUBE * v * v * v)))).astype(BF16).astype(F32)

    def strided(ref, start):
        return jnp.concatenate(
            [ref[t, pl.ds(start, rows, 2), :] for t in range(tiles)], axis=1
        )

    shifted = [strided(gf, PAD - 2 + j).astype(BF16) for j in range(taps + 1)]
    cots = [ct[PAD + d:PAD + d + rows, :].astype(BF16) for d in (-1, 0, 1)]

    even, odd = shifted[2], shifted[3]
    se = [dot(even, c, TN)[0:half] for c in cots]
    so = [dot(odd, c, TN)[0:half] for c in cots]
    for k, (e, o) in enumerate(((2, 2), (1, 2), (1, 1), (0, 1), (0, 0))):
        part = 0.5 * (se[e] + so[o])
        for t in range(ny):
            dwo[t, k] = part[:, 128 * t:128 * t + 128]
            dws[t, k] = part[:, 128 * t:128 * t + 128].astype(BF16)
    c_y = []
    for d in range(1, ny):
        c_y.append(send(dws.at[at_y(d)], yr.at[d - 1], s_y.at[d - 1], r_y.at[d - 1], device(z, x, core, at_y(d))))

    for c in c_az:
        c.wait_recv()
    for k in range(taps):
        for zz in range(nzl):
            wf[own * zz:own * (zz + 1)] = zb[zz, k].astype(F32)
        wx[x, k] = wf[...].astype(BF16)
    c_ax = []
    for d in range(1, nx):
        c_ax.append(send(wx.at[x], wx.at[x], s_ax.at[d - 1], r_ax.at[d - 1], device(z, at_x(d), core, y)))

    for c in c_y:
        c.wait_recv()
    for k in range(taps):
        total = dwo[y, k]
        for d in range(ny - 1):
            total = total + yr[d, k].astype(F32)
        for xx in range(nx):
            piece = total[block * xx:block * (xx + 1)]
            xo[xx, k] = piece
            xs[xx, k] = piece.astype(BF16)
    c_x = []
    for d in range(1, nx):
        c_x.append(send(xs.at[at_x(d)], xr.at[d - 1], s_x.at[d - 1], r_x.at[d - 1], device(z, at_x(d), core, y)))

    for c in c_ax:
        c.wait_recv()
    conv = jnp.zeros((rows, p.cout), F32)
    cot_all = ct[:, 0:p.cout].astype(BF16)
    for k in range(taps):
        w = wx[:, k].reshape(half, p.cout)
        conv = conv + dot(shifted[k][:, 0:half], w, NN)
        conv = conv + dot(shifted[k + 1][:, 0:half], w, NN)
        cks[k, :, 0:half] = dot(cot_all, w, NT)
        if half < p.halfp:
            cks[k, :, half:] = jnp.zeros((rows + 2 * PAD, p.halfp - half), F32)
    conv = 0.5 * conv
    for h in (0, 1):
        pf_s[h] = conv[pairs * h:pairs * (h + 1)]
    c_pf = send(pf_s.at[other], pf_r, s_loc.at[6], r_loc.at[6], partner)

    def shift(k, d):
        return cks[k, PAD + d:PAD + d + rows, :]

    grad_even = 0.5 * (shift(0, 1) + shift(1, 0) + shift(2, 0) + shift(3, -1) + shift(4, -1))
    grad_odd = 0.5 * (shift(0, 1) + shift(1, 1) + shift(2, 0) + shift(3, 0) + shift(4, -1))
    gain_part = jnp.zeros((1, p.halfp), F32)
    for start, grad in ((0, grad_even), (1, grad_odd)):
        a = strided(af, PAD + start)
        v = a * gain_half
        t = jnp.tanh(ROOT * (v + CUBE * v * v * v))
        slope = 0.5 * (1.0 + t) + 0.5 * v * (1.0 - t * t) * (ROOT * (1.0 + 3.0 * CUBE * v * v))
        pre = grad * slope
        gain_part = gain_part + jnp.sum(pre * a, axis=0, keepdims=True)
        out = pre * gain_half
        for tt in range(p.halfp // 128):
            io[tt, pl.ds(start, rows, 2), :] = out[:, 128 * tt:128 * tt + 128]
    for h in (0, 1):
        gi_s[h] = jnp.concatenate(
            [io[tt, rows * h:rows * (h + 1), :] for tt in range(p.halfp // 128)], axis=1
        ).astype(BF16)
    c_gi = send(gi_s.at[other], gi_r, s_loc.at[7], r_loc.at[7], partner)

    gt[...] = jnp.zeros_like(gt)
    for t in range(tiles):
        gt[0, t:t + 1, :] = gain_part[:, 128 * t:128 * t + 128]
    bias_part = jnp.sum(ct[pl.ds(pl.multiple_of(PAD + pairs * core, 8), pairs), :], axis=0, keepdims=True)
    for t in range(ny):
        gt[0, 4 + t:5 + t, :] = bias_part[:, 128 * t:128 * t + 128]
    c_gx = []
    for flip in (0, 1):
        for d in range(nx):
            if flip == 0 and d == 0:
                continue
            i = flip * nx + d
            cc = core if flip == 0 else other
            c_gx.append(send(gt.at[0], gx.at[i], s_gx.at[i], r_gx.at[i], device(z, at_x(d), cc, y)))

    for c in c_x:
        c.wait_recv()
    zo[...] = jnp.zeros_like(zo)
    for k in range(taps):
        wf2 = xo[x, k]
        for d in range(nx - 1):
            wf2 = wf2 + xr[d, k].astype(F32)
        for zz in range(nzl):
            zo[zz, own * k:own * (k + 1), :] = wf2[own * zz:own * (zz + 1)]
    zs[...] = zo[...].astype(BF16)
    c_z = []
    for d in range(1, nz):
        c_z.append(send(zs.at[at_z(d) % nzl], zr.at[d - 1], s_z.at[d - 1], r_z.at[d - 1], device(at_z(d), x, core, y)))

    for c in c_gx:
        c.wait_recv()
    same = gt[0]
    for d in range(1, nx):
        same = same + gx[d]
    flipped = gx[nx]
    for d in range(1, nx):
        flipped = flipped + gx[nx + d]
    first = jnp.where(core == 0, same, flipped)
    second = jnp.where(core == 0, flipped, same)
    gt[1, 0:2, :] = first[0:2]
    gt[1, 2:4, :] = second[0:2]
    gt[1, 4:8, :] = (first + second)[4:8]
    c_gy = []
    for d in range(1, ny):
        c_gy.append(send(gt.at[1], gy.at[d - 1], s_gy.at[d - 1], r_gy.at[d - 1], device(z, x, core, at_y(d))))
    for c in c_gy:
        c.wait_recv()
    total = gt[1]
    for d in range(ny - 1):
        total = total + gy[d]
    gs[...] = total
    c_gz = []
    for d in range(1, nz):
        c_gz.append(send(gs, gz.at[d - 1], s_gz.at[d - 1], r_gz.at[d - 1], device(at_z(d), x, core, y)))

    c_pf.wait_recv()
    pooled[0] = (pf_s[core] + pf_r[...] + bias[...]).astype(BF16)
    c_gi.wait_recv()
    grad_input[0] = (dot(gi_s[core], mine, NT) + dot(gi_r[...], sel[other], NT)).astype(BF16)

    for c in c_z:
        c.wait_recv()
    final = zo[z_lo]
    for d in range(nz - 1):
        final = final + zr[d].astype(F32)
    ya[y] = final * factor
    c_ya = []
    for d in range(1, ny):
        c_ya.append(send(ya.at[y], ya.at[y], s_ya.at[d - 1], r_ya.at[d - 1], device(z, x, core, at_y(d))))

    for c in c_gz:
        c.wait_recv()
    total = gs[...]
    for d in range(nz - 1):
        total = total + gz[d]
    total = total * factor
    halves = [
        jnp.concatenate([total[2 * h + t:2 * h + t + 1] for t in range(tiles)], axis=1) for h in (0, 1)
    ]
    summed = jnp.zeros((8, p.cin), F32)
    for h in (0, 1):
        wide = jnp.broadcast_to(halves[h], (8, p.halfp))
        summed = summed + dot(wide, sel[h].astype(F32), NT, HI)
    grad_gain[...] = summed[0:1]
    grad_bias[...] = jnp.concatenate([total[4 + t:5 + t] for t in range(ny)], axis=1)[:, 0:p.cout]

    for c in c_ya:
        c.wait_recv()
    for k in range(taps):
        wide = jnp.concatenate([ya[t, own * k:own * (k + 1), :] for t in range(ny)], axis=1)
        grad_weight[k] = wide[:, 0:p.cout]
    for c in started:
        c.wait_send()


def build(mesh, plan, factor):
    p = plan
    nx, ny, nz, nzl = p.nx, p.ny, p.nz, p.nzl
    pairs = p.rows // 2
    zrows = -(-p.own * p.taps // 16) * 16
    dma = pltpu.SemaphoreType.DMA
    sems = (8, len(p.offsets), nx - 1, ny - 1, nx - 1, nz - 1, ny - 1, 2 * nx, ny - 1, nz - 1)
    scratch = [
        pltpu.VMEM((p.rows, p.cin), BF16),
        pltpu.VMEM((pairs, p.cout), BF16),
        pltpu.VMEM((2, 16, p.cin), BF16),
        pltpu.VMEM((2, 16, p.cout), BF16),
        pltpu.VMEM((2, p.cin, p.halfp), BF16),
        pltpu.VMEM((p.halfp // 128, 2 * p.rows + 2 * PAD, 128), F32),
        pltpu.VMEM((p.halfp // 128, 2 * p.rows + 2 * PAD, 128), F32),
        pltpu.VMEM((p.rows + 2 * PAD, p.coutp), F32),
        pltpu.VMEM((nzl, p.taps, p.own, p.cout), BF16),
        pltpu.VMEM((p.block, p.cout), F32),
        pltpu.VMEM((nx, p.taps, p.block, p.cout), BF16),
        pltpu.VMEM((ny, p.taps, p.half, 128), BF16),
        pltpu.VMEM((ny, p.taps, p.half, 128), F32),
        pltpu.VMEM((ny - 1, p.taps, p.half, 128), BF16),
        pltpu.VMEM((nx, p.taps, p.block, 128), BF16),
        pltpu.VMEM((nx, p.taps, p.block, 128), F32),
        pltpu.VMEM((nx - 1, p.taps, p.block, 128), BF16),
        pltpu.VMEM((nzl, zrows, 128), F32),
        pltpu.VMEM((nzl, zrows, 128), BF16),
        pltpu.VMEM((nz - 1, zrows, 128), BF16),
        pltpu.VMEM((ny, zrows, 128), F32),
        pltpu.VMEM((p.taps, p.rows + 2 * PAD, p.halfp), F32),
        pltpu.VMEM((p.halfp // 128, 2 * p.rows, 128), F32),
        pltpu.VMEM((2, p.rows, p.halfp), BF16),
        pltpu.VMEM((p.rows, p.halfp), BF16),
        pltpu.VMEM((2, pairs, p.cout), F32),
        pltpu.VMEM((pairs, p.cout), F32),
        pltpu.VMEM((2 * nx, 8, 128), F32),
        pltpu.VMEM((2, 8, 128), F32),
        pltpu.VMEM((ny - 1, 8, 128), F32),
        pltpu.VMEM((8, 128), F32),
        pltpu.VMEM((nz - 1, 8, 128), F32),
    ]
    for n in sems:
        scratch += [dma((n,)), dma((n,))]
    vmem = pl.BlockSpec(memory_space=pltpu.VMEM)

    def per_device(activ, gain, weight, bias, cotangent):
        outs = pl.pallas_call(
            functools.partial(kernel, p, factor),
            out_shape=(
                jax.ShapeDtypeStruct((1, pairs, p.cout), BF16),
                jax.ShapeDtypeStruct((1, p.rows, p.cin), BF16),
                jax.ShapeDtypeStruct((p.taps, p.own, p.cout), F32),
                jax.ShapeDtypeStruct((1, p.cin), F32),
                jax.ShapeDtypeStruct((1, p.cout), F32),
            ),
            in_specs=[vmem] * 5,
            out_specs=(vmem,) * 5,
            scratch_shapes=scratch,
            compiler_params=pltpu.CompilerParams(collective_id=0, has_side_effects=True),
        )(activ, gain.reshape(1, -1), weight, bias.reshape(1, -1), cotangent)
        return (*outs[:3], outs[3].reshape(-1), outs[4].reshape(-1))

    in_specs = (P("batch", "seq", None), P(), P(None, "seq", None), P(), P("batch", "seq", None))
    out_specs = (P("batch", "seq", None), P("batch", "seq", None), P(None, "seq", None), P(), P())
    return jax.shard_map(per_device, mesh=mesh, in_specs=in_specs, out_specs=out_specs, check_vma=False)


def solution(mesh):
    return build(mesh, Plan(), float(8 * 8192) ** -0.5)
```

time: 353 us -> 64.5 us (0.18)
  the two profiles are of different devices: /device:TPU:32 before, /device:TPU:1 now
where the time goes in v1:
time: 64.5 us; the launch traced here: 64.2 us
  Pallas kernels  57.4 us (89%)
  local copies, waits for them, and re-layouts  4.89 us (8%)
  other arithmetic  1.31 us (2%)
  between operations  0.65 us (1%)
    pallas_call x1, Pallas kernels, per_device(): pl.pallas_call(functools.partial(kernel, p, factor), out_shape=(jax.Shape...  57.4 us
    unnamed x10, local copies, waits for them, and re-layouts  3.65 us
    pallas_call x1, other arithmetic, per_device(): pl.pallas_call(functools.partial(kernel, p, factor), out_shape=(jax.Shape...  1.31 us

profile of v1, /device:TPU:1, one launch (start us, length us, event | category | flops | bytes accessed | tf_op | source)
XLA Modules:
  0.0 64.2 jit_solution(7391256260676320831)
XLA Ops:
  0.6 1.2 %reshape.22.gain = f32[1,384]{1,0:T(1,128)} reshape(f32[384]{0:T(512)} %param.6) | data formatting | bytes 3072 | tf_op jit(solution)/shard_map/reshape | solution.py:431
  1.9 57.4 %shard_map.92 = (bf16[1,64,448]{2,1,0:T(8,128)(2,1)}, bf16[1,128,384]{2,1,0:T(8,128)(2,1)}, f32[5,6,448]{2,1,0:T(8,128)}, f32[1,384]{1,0:T(1,128)}, f32[1,448]{1,0:T(1,128)}) custom-call(bf16[1,128,384]{2,1,0:T(8,128)(2,1)} %activ.1, f32[1,384]{1,0:T(1,128)} %reshape.22.gain, bf16[5,6,448]{2,1,0:T(8,128)(2,1)} %weight.1, f32[1,448]{1,0:T(1,128)} %bitcast.2, ...), custom_call_target="tpu_custom_call" | custom-call | tf_op jit(solution)/shard_map/pallas_call | solution.py:418
  59.3 0.0 copy-start
  59.3 1.3 %reduce = f32[384]{0:T(512)} reduce(f32[1,384]{1,0:T(1,128)} %get-tuple-element.13, f32[]{:T(128)} %constant.3), dimensions={0}, to_apply=%get-tuple-element.13.reduce_sub_computation | reduce | bytes 3076 | tf_op jit(solution)/shard_map/pallas_call | solution.py:418
  60.6 1.5 %copy.14 = bf16[1,64,448]{2,1,0:T(8,128)(2,1)} copy(bf16[1,64,448]{2,1,0:T(8,128)(2,1)} %get-tuple-element.20) | data formatting | bytes 114688
  62.0 0.0 copy-done
  62.0 0.0 copy-start.1
  62.1 0.6 copy.15
  62.7 0.3 copy-done.1
  63.0 0.0 copy-start.2
  63.0 0.6 copy.16
  63.6 0.0 copy-done.2
  63.6 0.6 copy.17
Async XLA Ops:
  59.3 2.8 %copy-start = (bf16[1,128,384]{2,1,0:T(8,128)(2,1)S(1)}, bf16[1,128,384]{2,1,0:T(8,128)(2,1)}, u32[]{:S(2)}) copy-start(bf16[1,128,384]{2,1,0:T(8,128)(2,1)} %get-tuple-element.21) | copy-start | bytes 294916
  62.0 0.9 %copy-start.1 = (f32[5,6,448]{2,1,0:T(8,128)S(1)}, f32[5,6,448]{2,1,0:T(8,128)}, u32[]{:S(2)}) copy-start(f32[5,6,448]{2,1,0:T(8,128)} %get-tuple-element.22) | copy-start | bytes 161284
  63.0 0.7 %copy-start.2 = (f32[1,448]{1,0:T(1,128)S(1)}, f32[1,448]{1,0:T(1,128)}, u32[]{:S(2)}) copy-start(f32[1,448]{1,0:T(1,128)} %get-tuple-element.14) | copy-start | bytes 5380

commit v2 on v1

--- a/solution.py
+++ b/solution.py
@@ -11,7 +11,6 @@
 MESH = pl.DeviceIdType.MESH
 F32 = jnp.float32
 BF16 = jnp.bfloat16
-HI = lax.Precision.HIGHEST
 ROOT = 0.7978845608028654
 CUBE = 0.044715
 PAD = 8
@@ -58,22 +57,43 @@
         return tuple(range(1, far + 1)) + tuple(-o for o in range(1, self.nzl - far))
 
 
-def dot(a, b, dims, precision=None):
-    return lax.dot_general(a, b, (dims, ((), ())), precision=precision, preferred_element_type=F32)
+def dot(a, b, dims):
+    return lax.dot_general(a, b, (dims, ((), ())), preferred_element_type=F32)
+
+
+def picked(row, ones, dims):
+    first = row.astype(BF16)
+    rest = row - first.astype(F32)
+    second = rest.astype(BF16)
+    third = (rest - second.astype(F32)).astype(BF16)
+    pieces = [jnp.broadcast_to(v.astype(F32), (8, row.shape[1])) for v in (first, second, third)]
+    line = lax.broadcasted_iota(jnp.int32, pieces[0].shape, 0)
+    rows = jnp.where(line == 0, pieces[0], jnp.where(line == 1, pieces[1], jnp.where(line == 2, pieces[2], 0.0)))
+    out = dot(rows.astype(BF16), ones, dims)
+    return out[0:1] + out[1:2] + out[2:3]
 
 
 NN = ((1,), (0,))
 NT = ((1,), (1,))
 TN = ((0,), (0,))
+
+
+TAPS = (2, 1, 3, 0, 4)
+GROUPS = ((0, 16, (2, 1)), (16, 16, (3, 0)), (32, 8, (4,)))
+ORDER = (
+    ("wz", 0), ("wz", 1), ("wz", 2), ("ys", 0), ("wz", 3), ("wz", 4), ("cv", 0), ("ys", 1), ("cv", 1), ("ys", 2),
+    ("cv", 2), ("xs", 0), ("ys", 3), ("cv", 3), ("ys", 4), ("cv", 4),
+)
+LATE = (1, 2)
 
 
 def kernel(
     plan, factor,
     activ, gain, weight, bias, cot,
     pooled, grad_input, grad_weight, grad_gain, grad_bias,
-    act_p, cot_p, act_h, cot_h, sel, af, gf, ct, zb, wf, wx, dws, dwo, yr, xs, xo, xr, zo, zs, zr, ya,
-    cks, io, gi_s, gi_r, pf_s, pf_r, gx, gt, gy, gs, gz,
-    s_loc, r_loc, s_az, r_az, s_ax, r_ax, s_y, r_y, s_x, r_x, s_z, r_z, s_ya, r_ya, s_gx, r_gx, s_gy, r_gy, s_gz, r_gz,
+    act_p, cot_p, act_h, cot_h, sel, af, gf, ct, zb, wf, wx, dws, dwo, yr, xs, xo, xr, zo, zs0, zs1, zs2, zr0, zr1, zr2, ya,
+    cks, io, gi_s, gi_r, pf_s, pf_r, gx, gt, gs, gz,
+    s_loc, r_loc, s_az, r_az, s_ax, r_ax, s_y, r_y, s_x, r_x, s_z, r_z, s_ya, r_ya, s_gx, r_gx, s_gz, r_gz,
 ):
     p = plan
     nx, ny, nz, nzl = p.nx, p.ny, p.nz, p.nzl
@@ -121,12 +141,12 @@
     for peer in peers:
         pl.semaphore_signal(barrier, inc=1, device_id=peer, device_id_type=MESH)
 
-    q = lax.broadcasted_iota(jnp.int32, (p.cin, p.halfp), 1)
+    q = lax.broadcasted_iota(jnp.int32, (8, p.halfp), 1)
+    chan = own * ((q % block) // own * (2 * nx) + (q // block) * 2) + q % own
+    chan = jnp.where(q < half, chan, 2 * p.cin)[0:1]
     r = lax.broadcasted_iota(jnp.int32, (p.cin, p.halfp), 0)
-    chan = own * ((q % block) // own * (2 * nx) + (q // block) * 2) + q % own
-    valid = q < half
-    sel[0] = jnp.where(valid & (r == chan), 1.0, 0.0).astype(BF16)
-    sel[1] = jnp.where(valid & (r == chan + own), 1.0, 0.0).astype(BF16)
+    sel[0] = jnp.where(r == chan, 1.0, 0.0).astype(BF16)
+    sel[1] = jnp.where(r == chan + own, 1.0, 0.0).astype(BF16)
     mine = sel[core]
 
     ct[...] = jnp.zeros_like(ct)
@@ -138,7 +158,7 @@
 
     put(pl.multiple_of(PAD + rows * core, 8), dot(activ[0], mine, NN))
     ct[pl.ds(pl.multiple_of(PAD + pairs * core, 8), pairs), 0:p.cout] = cot[0].astype(F32)
-    gain_half = dot(jnp.broadcast_to(gain[...], (8, p.cin)), mine.astype(F32), NN, HI)[0:1]
+    gain_half = picked(gain[...], mine, NN)
 
     pl.semaphore_wait(barrier, len(peers))
 
@@ -164,16 +184,48 @@
         to = chip_core(up_chip, cc)
         halos.append(send(activ.at[0, a_edge], act_h.at[side], s_loc.at[2 + i], r_loc.at[2 + side], to))
         halos.append(send(cot.at[0, c_edge], cot_h.at[side], s_loc.at[4 + i], r_loc.at[4 + side], to))
+    n_off = len(p.offsets)
     c_az = []
-    for i, o in enumerate(p.offsets):
-        to = device(at_z(sign * o), x, core, y)
-        c_az.append(send(weight, zb.at[z_lo], s_az.at[i], r_az.at[i], to))
+    for k in range(taps):
+        for i, o in enumerate(p.offsets):
+            j = k * n_off + i
+            c_az.append(send(weight.at[k], zb.at[z_lo, k], s_az.at[j], r_az.at[j], device(at_z(sign * o), x, core, y)))
     zb[z_lo] = weight[...]
+
+    def activate(start, count):
+        for t in range(tiles):
+            v = af[t, start:start + count, :] * gain_half[:, 128 * t:128 * t + 128]
+            gf[t, start:start + count, :] = (
+                0.5 * v * (1.0 + jnp.tanh(ROOT * (v + CUBE * v * v * v)))
+            ).astype(BF16).astype(F32)
+
+    def strided(ref, start):
+        return jnp.concatenate([ref[t, pl.ds(start, rows, 2), :] for t in range(tiles)], axis=1)
+
+    def cot_shift(d):
+        return ct[PAD + d:PAD + d + rows, :].astype(BF16)
+
+    c_y = [None] * taps
+
+    def y_send(k, part):
+        for t in range(ny):
+            dwo[t, k] = part[:, 128 * t:128 * t + 128]
+            dws[t, k] = part[:, 128 * t:128 * t + 128].astype(BF16)
+        c_y[k] = []
+        for d in range(1, ny):
+            i = (ny - 1) * k + d - 1
+            c_y[k].append(send(dws.at[at_y(d), k], yr.at[d - 1, k], s_y.at[i], r_y.at[i], device(z, x, core, at_y(d))))
 
     c_act.wait_recv()
     put(pl.multiple_of(PAD + rows * other, 8), dot(act_p[...], mine, NN))
     c_cot.wait_recv()
     ct[pl.ds(pl.multiple_of(PAD + pairs * other, 8), pairs), 0:p.cout] = cot_p[...].astype(F32)
+    activate(PAD, 2 * rows)
+    even, odd = strided(gf, PAD).astype(BF16), strided(gf, PAD + 1).astype(BF16)
+    here = cot_shift(0)
+    e0, o0 = dot(even, here, TN)[0:half], dot(odd, here, TN)[0:half]
+    y_send(2, 0.5 * (e0 + o0))
+
     for s in (0, 1):
         for src, dst, i in ((activ.at[0, a_edge], act_h, 2), (cot.at[0, c_edge], cot_h, 4)):
             pltpu.make_async_remote_copy(
@@ -183,48 +235,38 @@
     place = z_lo * nx + x
     before = jnp.where(place > 0, 1.0, 0.0).astype(F32)
     after = jnp.where(place < nzl * nx - 1, 1.0, 0.0).astype(F32)
+    ct[0:PAD, 0:p.cout] = (cot_h[1].astype(F32) * before)[edge - PAD:edge]
+    ct[PAD + rows:, 0:p.cout] = (cot_h[0].astype(F32) * after)[0:PAD]
+    up, down = cot_shift(1), cot_shift(-1)
+    o_up = dot(odd, up, TN)[0:half]
+    y_send(1, 0.5 * (e0 + o_up))
+    e_down = dot(even, down, TN)[0:half]
+    y_send(3, 0.5 * (e_down + o0))
+    y_send(0, 0.5 * (dot(even, up, TN)[0:half] + o_up))
+    y_send(4, 0.5 * (e_down + dot(odd, down, TN)[0:half]))
     put(0, (dot(act_h[1], mine, NN) * before)[edge - PAD:edge])
     put(PAD + 2 * rows, (dot(act_h[0], mine, NN) * after)[0:PAD])
-    ct[0:PAD, 0:p.cout] = (cot_h[1].astype(F32) * before)[edge - PAD:edge]
-    ct[PAD + rows:, 0:p.cout] = (cot_h[0].astype(F32) * after)[0:PAD]
-
-    for t in range(tiles):
-        v = af[t] * gain_half[:, 128 * t:128 * t + 128]
-        gf[t] = (0.5 * v * (1.0 + jnp.tanh(ROOT * (v + CUBE * v * v * v)))).astype(BF16).astype(F32)
-
-    def strided(ref, start):
-        return jnp.concatenate(
-            [ref[t, pl.ds(start, rows, 2), :] for t in range(tiles)], axis=1
-        )
-
-    shifted = [strided(gf, PAD - 2 + j).astype(BF16) for j in range(taps + 1)]
-    cots = [ct[PAD + d:PAD + d + rows, :].astype(BF16) for d in (-1, 0, 1)]
-
-    even, odd = shifted[2], shifted[3]
-    se = [dot(even, c, TN)[0:half] for c in cots]
-    so = [dot(odd, c, TN)[0:half] for c in cots]
-    for k, (e, o) in enumerate(((2, 2), (1, 2), (1, 1), (0, 1), (0, 0))):
-        part = 0.5 * (se[e] + so[o])
-        for t in range(ny):
-            dwo[t, k] = part[:, 128 * t:128 * t + 128]
-            dws[t, k] = part[:, 128 * t:128 * t + 128].astype(BF16)
-    c_y = []
-    for d in range(1, ny):
-        c_y.append(send(dws.at[at_y(d)], yr.at[d - 1], s_y.at[d - 1], r_y.at[d - 1], device(z, x, core, at_y(d))))
-
-    for c in c_az:
-        c.wait_recv()
-    for k in range(taps):
+    activate(0, PAD)
+    activate(PAD + 2 * rows, PAD)
+
+    c_ax = []
+
+    def weights_z(k):
+        for c in c_az[n_off * k:n_off * (k + 1)]:
+            c.wait_recv()
         for zz in range(nzl):
-            wf[own * zz:own * (zz + 1)] = zb[zz, k].astype(F32)
-        wx[x, k] = wf[...].astype(BF16)
-    c_ax = []
-    for d in range(1, nx):
-        c_ax.append(send(wx.at[x], wx.at[x], s_ax.at[d - 1], r_ax.at[d - 1], device(z, at_x(d), core, y)))
-
-    for c in c_y:
-        c.wait_recv()
-    for k in range(taps):
+            wf[k % 2, own * zz:own * (zz + 1)] = zb[zz, k].astype(F32)
+        wx[x, k] = wf[k % 2].astype(BF16)
+        for d in range(1, nx):
+            i = (nx - 1) * k + d - 1
+            c_ax.append(send(wx.at[x, k], wx.at[x, k], s_ax.at[i], r_ax.at[i], device(z, at_x(d), core, y)))
+
+    c_x = {}
+
+    def y_sum(n):
+        k = TAPS[n]
+        for c in c_y[k]:
+            c.wait_recv()
         total = dwo[y, k]
         for d in range(ny - 1):
             total = total + yr[d, k].astype(F32)
@@ -232,21 +274,49 @@
             piece = total[block * xx:block * (xx + 1)]
             xo[xx, k] = piece
             xs[xx, k] = piece.astype(BF16)
-    c_x = []
-    for d in range(1, nx):
-        c_x.append(send(xs.at[at_x(d)], xr.at[d - 1], s_x.at[d - 1], r_x.at[d - 1], device(z, at_x(d), core, y)))
-
-    for c in c_ax:
-        c.wait_recv()
-    conv = jnp.zeros((rows, p.cout), F32)
+        c_x[k] = []
+        for d in range(1, nx):
+            i = (nx - 1) * k + d - 1
+            c_x[k].append(send(xs.at[at_x(d), k], xr.at[d - 1, k], s_x.at[i], r_x.at[i], device(z, at_x(d), core, y)))
+
+    z_s, z_r = (zs0, zs1, zs2), (zr0, zr1, zr2)
+    c_z = []
+
+    def x_sum(g):
+        base, length, members = GROUPS[g]
+        zo[:, base:base + length, :] = jnp.zeros((nzl, length, 128), F32)
+        for n, k in enumerate(members):
+            for c in c_x[k]:
+                c.wait_recv()
+            total = xo[x, k]
+            for d in range(nx - 1):
+                total = total + xr[d, k].astype(F32)
+            for zz in range(nzl):
+                zo[zz, base + own * n:base + own * (n + 1), :] = total[own * zz:own * (zz + 1)]
+        z_s[g][...] = zo[:, base:base + length, :].astype(BF16)
+        for d in range(1, nz):
+            i = (nz - 1) * g + d - 1
+            c_z.append(
+                send(z_s[g].at[at_z(d) % nzl], z_r[g].at[d - 1], s_z.at[i], r_z.at[i], device(at_z(d), x, core, y))
+            )
+
+    acc = [None]
     cot_all = ct[:, 0:p.cout].astype(BF16)
-    for k in range(taps):
+    shifted = [strided(gf, PAD - 2 + j)[:, 0:half].astype(BF16) for j in range(taps + 1)]
+
+    def convs(k):
+        for c in c_ax[(nx - 1) * k:(nx - 1) * (k + 1)]:
+            c.wait_recv()
         w = wx[:, k].reshape(half, p.cout)
-        conv = conv + dot(shifted[k][:, 0:half], w, NN)
-        conv = conv + dot(shifted[k + 1][:, 0:half], w, NN)
+        add = dot(shifted[k], w, NN) + dot(shifted[k + 1], w, NN)
+        acc[0] = add if acc[0] is None else acc[0] + add
         cks[k, :, 0:half] = dot(cot_all, w, NT)
         if half < p.halfp:
             cks[k, :, half:] = jnp.zeros((rows + 2 * PAD, p.halfp - half), F32)
+
+    for step, k in ORDER:
+        {"wz": weights_z, "ys": y_sum, "cv": convs, "xs": x_sum}[step](k)
+    conv = acc[0]
     conv = 0.5 * conv
     for h in (0, 1):
         pf_s[h] = conv[pairs * h:pairs * (h + 1)]
@@ -282,49 +352,29 @@
         gt[0, 4 + t:5 + t, :] = bias_part[:, 128 * t:128 * t + 128]
     c_gx = []
     for flip in (0, 1):
-        for d in range(nx):
-            if flip == 0 and d == 0:
-                continue
-            i = flip * nx + d
-            cc = core if flip == 0 else other
-            c_gx.append(send(gt.at[0], gx.at[i], s_gx.at[i], r_gx.at[i], device(z, at_x(d), cc, y)))
-
-    for c in c_x:
-        c.wait_recv()
-    zo[...] = jnp.zeros_like(zo)
-    for k in range(taps):
-        wf2 = xo[x, k]
-        for d in range(nx - 1):
-            wf2 = wf2 + xr[d, k].astype(F32)
-        for zz in range(nzl):
-            zo[zz, own * k:own * (k + 1), :] = wf2[own * zz:own * (zz + 1)]
-    zs[...] = zo[...].astype(BF16)
-    c_z = []
-    for d in range(1, nz):
-        c_z.append(send(zs.at[at_z(d) % nzl], zr.at[d - 1], s_z.at[d - 1], r_z.at[d - 1], device(at_z(d), x, core, y)))
+        for dy in range(ny):
+            for dx in range(nx):
+                i = (flip * ny + dy) * nx + dx
+                if i > 0:
+                    cc = core if flip == 0 else other
+                    c_gx.append(send(gt.at[0], gx.at[i], s_gx.at[i], r_gx.at[i], device(z, at_x(dx), cc, at_y(dy))))
+
+    for g in LATE:
+        x_sum(g)
 
     for c in c_gx:
         c.wait_recv()
     same = gt[0]
-    for d in range(1, nx):
-        same = same + gx[d]
-    flipped = gx[nx]
-    for d in range(1, nx):
-        flipped = flipped + gx[nx + d]
+    for i in range(1, ny * nx):
+        same = same + gx[i]
+    flipped = gx[ny * nx]
+    for i in range(1, ny * nx):
+        flipped = flipped + gx[ny * nx + i]
     first = jnp.where(core == 0, same, flipped)
     second = jnp.where(core == 0, flipped, same)
-    gt[1, 0:2, :] = first[0:2]
-    gt[1, 2:4, :] = second[0:2]
-    gt[1, 4:8, :] = (first + second)[4:8]
-    c_gy = []
-    for d in range(1, ny):
-        c_gy.append(send(gt.at[1], gy.at[d - 1], s_gy.at[d - 1], r_gy.at[d - 1], device(z, x, core, at_y(d))))
-    for c in c_gy:
-        c.wait_recv()
-    total = gt[1]
-    for d in range(ny - 1):
-        total = total + gy[d]
-    gs[...] = total
+    gs[0:2, :] = first[0:2]
+    gs[2:4, :] = second[0:2]
+    gs[4:8, :] = (first + second)[4:8]
     c_gz = []
     for d in range(1, nz):
         c_gz.append(send(gs, gz.at[d - 1], s_gz.at[d - 1], r_gz.at[d - 1], device(at_z(d), x, core, y)))
@@ -336,10 +386,11 @@
 
     for c in c_z:
         c.wait_recv()
-    final = zo[z_lo]
-    for d in range(nz - 1):
-        final = final + zr[d].astype(F32)
-    ya[y] = final * factor
+    for g, (base, length, members) in enumerate(GROUPS):
+        final = zo[z_lo, base:base + length, :]
+        for d in range(nz - 1):
+            final = final + z_r[g][d].astype(F32)
+        ya[y, base:base + length, :] = final * factor
     c_ya = []
     for d in range(1, ny):
         c_ya.append(send(ya.at[y], ya.at[y], s_ya.at[d - 1], r_ya.at[d - 1], device(z, x, core, at_y(d))))
@@ -353,18 +404,16 @@
     halves = [
         jnp.concatenate([total[2 * h + t:2 * h + t + 1] for t in range(tiles)], axis=1) for h in (0, 1)
     ]
-    summed = jnp.zeros((8, p.cin), F32)
-    for h in (0, 1):
-        wide = jnp.broadcast_to(halves[h], (8, p.halfp))
-        summed = summed + dot(wide, sel[h].astype(F32), NT, HI)
-    grad_gain[...] = summed[0:1]
+    grad_gain[...] = picked(halves[0], sel[0], NT) + picked(halves[1], sel[1], NT)
     grad_bias[...] = jnp.concatenate([total[4 + t:5 + t] for t in range(ny)], axis=1)[:, 0:p.cout]
 
     for c in c_ya:
         c.wait_recv()
-    for k in range(taps):
-        wide = jnp.concatenate([ya[t, own * k:own * (k + 1), :] for t in range(ny)], axis=1)
-        grad_weight[k] = wide[:, 0:p.cout]
+    for base, length, members in GROUPS:
+        for n, k in enumerate(members):
+            row = base + own * n
+            wide = jnp.concatenate([ya[t, row:row + own, :] for t in range(ny)], axis=1)
+            grad_weight[k] = wide[:, 0:p.cout]
     for c in started:
         c.wait_send()
 
@@ -373,9 +422,12 @@
     p = plan
     nx, ny, nz, nzl = p.nx, p.ny, p.nz, p.nzl
     pairs = p.rows // 2
-    zrows = -(-p.own * p.taps // 16) * 16
+    zrows = sum(length for _, length, _ in GROUPS)
     dma = pltpu.SemaphoreType.DMA
-    sems = (8, len(p.offsets), nx - 1, ny - 1, nx - 1, nz - 1, ny - 1, 2 * nx, ny - 1, nz - 1)
+    sems = (
+        8, p.taps * len(p.offsets), p.taps * (nx - 1), p.taps * (ny - 1), p.taps * (nx - 1),
+        len(GROUPS) * (nz - 1), ny - 1, 2 * nx * ny, nz - 1,
+    )
     scratch = [
         pltpu.VMEM((p.rows, p.cin), BF16),
         pltpu.VMEM((pairs, p.cout), BF16),
@@ -386,7 +438,7 @@
         pltpu.VMEM((p.halfp // 128, 2 * p.rows + 2 * PAD, 128), F32),
         pltpu.VMEM((p.rows + 2 * PAD, p.coutp), F32),
         pltpu.VMEM((nzl, p.taps, p.own, p.cout), BF16),
-        pltpu.VMEM((p.block, p.cout), F32),
+        pltpu.VMEM((2, p.block, p.cout), F32),
         pltpu.VMEM((nx, p.taps, p.block, p.cout), BF16),
         pltpu.VMEM((ny, p.taps, p.half, 128), BF16),
         pltpu.VMEM((ny, p.taps, p.half, 128), F32),
@@ -395,8 +447,8 @@
         pltpu.VMEM((nx, p.taps, p.block, 128), F32),
         pltpu.VMEM((nx - 1, p.taps, p.block, 128), BF16),
         pltpu.VMEM((nzl, zrows, 128), F32),
-        pltpu.VMEM((nzl, zrows, 128), BF16),
-        pltpu.VMEM((nz - 1, zrows, 128), BF16),
+        *[pltpu.VMEM((nzl, length, 128), BF16) for _, length, _ in GROUPS],
+        *[pltpu.VMEM((nz - 1, length, 128), BF16) for _, length, _ in GROUPS],
         pltpu.VMEM((ny, zrows, 128), F32),
         pltpu.VMEM((p.taps, p.rows + 2 * PAD, p.halfp), F32),
         pltpu.VMEM((p.halfp // 128, 2 * p.rows, 128), F32),
@@ -404,9 +456,8 @@
         pltpu.VMEM((p.rows, p.halfp), BF16),
         pltpu.VMEM((2, pairs, p.cout), F32),
         pltpu.VMEM((pairs, p.cout), F32),
-        pltpu.VMEM((2 * nx, 8, 128), F32),
-        pltpu.VMEM((2, 8, 128), F32),
-        pltpu.VMEM((ny - 1, 8, 128), F32),
+        pltpu.VMEM((2 * nx * ny, 8, 128), F32),
+        pltpu.VMEM((1, 8, 128), F32),
         pltpu.VMEM((8, 128), F32),
         pltpu.VMEM((nz - 1, 8, 128), F32),
     ]

time: 64.5 us -> 63.4 us (0.983); the launches traced: 64.2 us -> 62.3 us
  Pallas kernels: 57.4 us -> 55.5 us
    pallas_call x1, Pallas kernels: 57.4 us -> 55.5 us  [per_device(): pl.pallas_call(functools.partial(kernel, p, factor), out_shape=(jax.Shape...]
where the time goes in v2:
time: 63.4 us; the launch traced here: 62.3 us
  Pallas kernels  55.5 us (88%)
  local copies, waits for them, and re-layouts  4.89 us (8%)
  other arithmetic  1.31 us (2%)
  between operations  0.65 us (1%)
    pallas_call x1, Pallas kernels, per_device(): pl.pallas_call(functools.partial(kernel, p, factor), out_shape=(jax.Shape...  55.5 us
    unnamed x10, local copies, waits for them, and re-layouts  3.65 us
    pallas_call x1, other arithmetic, per_device(): pl.pallas_call(functools.partial(kernel, p, factor), out_shape=(jax.Shape...  1.31 us

profile of v2, /device:TPU:1, one launch (start us, length us, event | category | flops | bytes accessed | tf_op | source)
XLA Modules:
  0.0 62.3 jit_solution(12958066650818014056)
XLA Ops:
  0.6 1.2 %reshape.22.gain = f32[1,384]{1,0:T(1,128)} reshape(f32[384]{0:T(512)} %param.6) | data formatting | bytes 3072 | tf_op jit(solution)/shard_map/reshape | solution.py:482
  1.9 55.5 %shard_map.92 = (bf16[1,64,448]{2,1,0:T(8,128)(2,1)}, bf16[1,128,384]{2,1,0:T(8,128)(2,1)}, f32[5,6,448]{2,1,0:T(8,128)}, f32[1,384]{1,0:T(1,128)}, f32[1,448]{1,0:T(1,128)}) custom-call(bf16[1,128,384]{2,1,0:T(8,128)(2,1)} %activ.1, f32[1,384]{1,0:T(1,128)} %reshape.22.gain, bf16[5,6,448]{2,1,0:T(8,128)(2,1)} %weight.1, f32[1,448]{1,0:T(1,128)} %bitcast.2, ...), custom_call_target="tpu_custom_call" | custom-call | tf_op jit(solution)/shard_map/pallas_call | solution.py:469
  57.3 0.0 copy-start
  57.4 1.3 %reduce = f32[384]{0:T(512)} reduce(f32[1,384]{1,0:T(1,128)} %get-tuple-element.13, f32[]{:T(128)} %constant.3), dimensions={0}, to_apply=%get-tuple-element.13.reduce_sub_computation | reduce | bytes 3076 | tf_op jit(solution)/shard_map/pallas_call | solution.py:469
  58.7 1.5 %copy.14 = bf16[1,64,448]{2,1,0:T(8,128)(2,1)} copy(bf16[1,64,448]{2,1,0:T(8,128)(2,1)} %get-tuple-element.20) | data formatting | bytes 114688
  60.1 0.0 copy-done
  60.1 0.0 copy-start.1
  60.1 0.6 %copy.15 = bf16[1,128,384]{2,1,0:T(8,128)(2,1)} copy(bf16[1,128,384]{2,1,0:T(8,128)(2,1)S(1)} %copy-done) | data formatting | bytes 196608
  60.8 0.3 copy-done.1
  61.1 0.0 copy-start.2
  61.1 0.6 %copy.16 = f32[5,6,448]{2,1,0:T(8,128)} copy(f32[5,6,448]{2,1,0:T(8,128)S(1)} %copy-done.1) | data formatting | bytes 107520
  61.7 0.0 copy-done.2
  61.7 0.6 copy.17
Async XLA Ops:
  57.3 2.8 %copy-start = (bf16[1,128,384]{2,1,0:T(8,128)(2,1)S(1)}, bf16[1,128,384]{2,1,0:T(8,128)(2,1)}, u32[]{:S(2)}) copy-start(bf16[1,128,384]{2,1,0:T(8,128)(2,1)} %get-tuple-element.21) | copy-start | bytes 294916
  60.1 0.9 %copy-start.1 = (f32[5,6,448]{2,1,0:T(8,128)S(1)}, f32[5,6,448]{2,1,0:T(8,128)}, u32[]{:S(2)}) copy-start(f32[5,6,448]{2,1,0:T(8,128)} %get-tuple-element.22) | copy-start | bytes 161284
  61.1 0.7 %copy-start.2 = (f32[1,448]{1,0:T(1,128)S(1)}, f32[1,448]{1,0:T(1,128)}, u32[]{:S(2)}) copy-start(f32[1,448]{1,0:T(1,128)} %get-tuple-element.14) | copy-start | bytes 5380

commit v3 on v2

--- a/solution.py
+++ b/solution.py
@@ -79,21 +79,22 @@
 
 
 TAPS = (2, 1, 3, 0, 4)
-GROUPS = ((0, 16, (2, 1)), (16, 16, (3, 0)), (32, 8, (4,)))
+GROUPS = ((0, 24, (2, 1, 3, 0)), (24, 8, (4,)))
+VIA_Z = (3, 4)
 ORDER = (
-    ("wz", 0), ("wz", 1), ("wz", 2), ("ys", 0), ("wz", 3), ("wz", 4), ("cv", 0), ("ys", 1), ("cv", 1), ("ys", 2),
-    ("cv", 2), ("xs", 0), ("ys", 3), ("cv", 3), ("ys", 4), ("cv", 4),
+    ("xf", 0), ("xf", 1), ("wz", 0), ("wz", 1), ("wz", 2), ("ys", 0), ("ys", 1), ("cv", 0), ("ys", 2), ("cv", 1),
+    ("ys", 3), ("cv", 2), ("ys", 4), ("zf", 0), ("cv", 3), ("zf", 1), ("cv", 4),
 )
-LATE = (1, 2)
+LATE = (0, 1)
 
 
 def kernel(
     plan, factor,
-    activ, gain, weight, bias, cot,
+    activ_h, gain_h, weight_h, bias_h, cot_h_,
     pooled, grad_input, grad_weight, grad_gain, grad_bias,
-    act_p, cot_p, act_h, cot_h, sel, af, gf, ct, zb, wf, wx, dws, dwo, yr, xs, xo, xr, zo, zs0, zs1, zs2, zr0, zr1, zr2, ya,
+    activ, gain, weight, bias, cot, s_in, act_p, cot_p, act_h, cot_h, sel, af, gf, ct, zb, wf, wx, dws, dwo, yr, xs, xo, xr, zo, zs0, zs1, zr0, zr1, ya, xb, xp, zx, wg, wh,
     cks, io, gi_s, gi_r, pf_s, pf_r, gx, gt, gs, gz,
-    s_loc, r_loc, s_az, r_az, s_ax, r_ax, s_y, r_y, s_x, r_x, s_z, r_z, s_ya, r_ya, s_gx, r_gx, s_gz, r_gz,
+    s_loc, r_loc, s_az, r_az, s_ax, r_ax, s_y, r_y, s_x, r_x, s_z, r_z, s_ya, r_ya, s_gx, r_gx, s_gz, r_gz, s_xf, r_xf, s_zf, r_zf,
 ):
     p = plan
     nx, ny, nz, nzl = p.nx, p.ny, p.nz, p.nzl
@@ -141,6 +142,14 @@
     for peer in peers:
         pl.semaphore_signal(barrier, inc=1, device_id=peer, device_id_type=MESH)
 
+    loads = [
+        pltpu.make_async_copy(src, dst, s_in.at[i])
+        for i, (src, dst) in enumerate(
+            ((activ_h.at[0], activ.at[0]), (gain_h, gain), (weight_h, weight), (bias_h, bias), (cot_h_.at[0], cot.at[0]))
+        )
+    ]
+    for load in loads:
+        load.start()
     q = lax.broadcasted_iota(jnp.int32, (8, p.halfp), 1)
     chan = own * ((q % block) // own * (2 * nx) + (q // block) * 2) + q % own
     chan = jnp.where(q < half, chan, 2 * p.cin)[0:1]
@@ -150,6 +159,8 @@
     mine = sel[core]
 
     ct[...] = jnp.zeros_like(ct)
+    for load in loads:
+        load.wait()
     tiles = p.halfp // 128
 
     def put(start, value):
@@ -158,7 +169,7 @@
 
     put(pl.multiple_of(PAD + rows * core, 8), dot(activ[0], mine, NN))
     ct[pl.ds(pl.multiple_of(PAD + pairs * core, 8), pairs), 0:p.cout] = cot[0].astype(F32)
-    gain_half = picked(gain[...], mine, NN)
+    gain_half = picked(gain[...].reshape(1, p.cin), mine, NN)
 
     pl.semaphore_wait(barrier, len(peers))
 
@@ -186,7 +197,13 @@
         halos.append(send(cot.at[0, c_edge], cot_h.at[side], s_loc.at[4 + i], r_loc.at[4 + side], to))
     n_off = len(p.offsets)
     c_az = []
-    for k in range(taps):
+    c_xf = []
+    for n, k in enumerate(VIA_Z):
+        for d in range(1, nx):
+            j = (nx - 1) * n + d - 1
+            c_xf.append(send(weight.at[k], xb.at[n, x], s_xf.at[j], r_xf.at[j], device(z, at_x(d), core, y)))
+        xb[n, x] = weight[k]
+    for k in range(taps - len(VIA_Z)):
         for i, o in enumerate(p.offsets):
             j = k * n_off + i
             c_az.append(send(weight.at[k], zb.at[z_lo, k], s_az.at[j], r_az.at[j], device(at_z(sign * o), x, core, y)))
@@ -261,6 +278,29 @@
             i = (nx - 1) * k + d - 1
             c_ax.append(send(wx.at[x, k], wx.at[x, k], s_ax.at[i], r_ax.at[i], device(z, at_x(d), core, y)))
 
+    c_zf = []
+
+    def weights_x(n):
+        for c in c_xf[(nx - 1) * n:(nx - 1) * (n + 1)]:
+            c.wait_recv()
+        for xx in range(nx):
+            wg[n, own * xx:own * (xx + 1)] = xb[n, xx].astype(F32)
+        xp[n] = wg[n].astype(BF16)
+        for i, o in enumerate(p.offsets):
+            j = n * n_off + i
+            c_zf.append(send(xp.at[n], zx.at[n, z_lo], s_zf.at[j], r_zf.at[j], device(at_z(sign * o), x, core, y)))
+        zx[n, z_lo] = xp[n]
+
+    def weights_last(n):
+        for c in c_zf[n_off * n:n_off * (n + 1)]:
+            c.wait_recv()
+        for zz in range(nzl):
+            rows_z = zx[n, zz].astype(F32)
+            for xx in range(nx):
+                wh[xx, own * zz:own * (zz + 1)] = rows_z[own * xx:own * (xx + 1)]
+        for xx in range(nx):
+            wx[xx, VIA_Z[n]] = wh[xx].astype(BF16)
+
     c_x = {}
 
     def y_sum(n):
@@ -279,7 +319,7 @@
             i = (nx - 1) * k + d - 1
             c_x[k].append(send(xs.at[at_x(d), k], xr.at[d - 1, k], s_x.at[i], r_x.at[i], device(z, at_x(d), core, y)))
 
-    z_s, z_r = (zs0, zs1, zs2), (zr0, zr1, zr2)
+    z_s, z_r = (zs0, zs1), (zr0, zr1)
     c_z = []
 
     def x_sum(g):
@@ -305,8 +345,9 @@
     shifted = [strided(gf, PAD - 2 + j)[:, 0:half].astype(BF16) for j in range(taps + 1)]
 
     def convs(k):
-        for c in c_ax[(nx - 1) * k:(nx - 1) * (k + 1)]:
-            c.wait_recv()
+        if k not in VIA_Z:
+            for c in c_ax[(nx - 1) * k:(nx - 1) * (k + 1)]:
+                c.wait_recv()
         w = wx[:, k].reshape(half, p.cout)
         add = dot(shifted[k], w, NN) + dot(shifted[k + 1], w, NN)
         acc[0] = add if acc[0] is None else acc[0] + add
@@ -315,7 +356,7 @@
             cks[k, :, half:] = jnp.zeros((rows + 2 * PAD, p.halfp - half), F32)
 
     for step, k in ORDER:
-        {"wz": weights_z, "ys": y_sum, "cv": convs, "xs": x_sum}[step](k)
+        {"wz": weights_z, "ys": y_sum, "cv": convs, "xs": x_sum, "xf": weights_x, "zf": weights_last}[step](k)
     conv = acc[0]
     conv = 0.5 * conv
     for h in (0, 1):
@@ -380,7 +421,7 @@
         c_gz.append(send(gs, gz.at[d - 1], s_gz.at[d - 1], r_gz.at[d - 1], device(at_z(d), x, core, y)))
 
     c_pf.wait_recv()
-    pooled[0] = (pf_s[core] + pf_r[...] + bias[...]).astype(BF16)
+    pooled[0] = (pf_s[core] + pf_r[...] + bias[...].reshape(1, p.cout)).astype(BF16)
     c_gi.wait_recv()
     grad_input[0] = (dot(gi_s[core], mine, NT) + dot(gi_r[...], sel[other], NT)).astype(BF16)
 
@@ -404,8 +445,8 @@
     halves = [
         jnp.concatenate([total[2 * h + t:2 * h + t + 1] for t in range(tiles)], axis=1) for h in (0, 1)
     ]
-    grad_gain[...] = picked(halves[0], sel[0], NT) + picked(halves[1], sel[1], NT)
-    grad_bias[...] = jnp.concatenate([total[4 + t:5 + t] for t in range(ny)], axis=1)[:, 0:p.cout]
+    grad_gain[...] = (picked(halves[0], sel[0], NT) + picked(halves[1], sel[1], NT)).reshape(p.cin)
+    grad_bias[...] = jnp.concatenate([total[4 + t:5 + t] for t in range(ny)], axis=1)[:, 0:p.cout].reshape(p.cout)
 
     for c in c_ya:
         c.wait_recv()
@@ -418,6 +459,11 @@
         c.wait_send()
 
 
+def hand_over(*refs):
+    for src, dst in zip(refs[:5], refs[5:]):
+        dst[...] = src[...]
+
+
 def build(mesh, plan, factor):
     p = plan
     nx, ny, nz, nzl = p.nx, p.ny, p.nz, p.nzl
@@ -427,8 +473,15 @@
     sems = (
         8, p.taps * len(p.offsets), p.taps * (nx - 1), p.taps * (ny - 1), p.taps * (nx - 1),
         len(GROUPS) * (nz - 1), ny - 1, 2 * nx * ny, nz - 1,
+        len(VIA_Z) * (nx - 1), len(VIA_Z) * len(p.offsets),
     )
     scratch = [
+        pltpu.VMEM((1, p.rows, p.cin), BF16),
+        pltpu.VMEM((p.cin,), F32),
+        pltpu.VMEM((p.taps, p.own, p.cout), BF16),
+        pltpu.VMEM((p.cout,), F32),
+        pltpu.VMEM((1, pairs, p.cout), BF16),
+        dma((5,)),
         pltpu.VMEM((p.rows, p.cin), BF16),
         pltpu.VMEM((pairs, p.cout), BF16),
         pltpu.VMEM((2, 16, p.cin), BF16),
@@ -450,6 +503,11 @@
         *[pltpu.VMEM((nzl, length, 128), BF16) for _, length, _ in GROUPS],
         *[pltpu.VMEM((nz - 1, length, 128), BF16) for _, length, _ in GROUPS],
         pltpu.VMEM((ny, zrows, 128), F32),
+        pltpu.VMEM((len(VIA_Z), nx, p.own, p.cout), BF16),
+        pltpu.VMEM((len(VIA_Z), p.own * nx, p.cout), BF16),
+        pltpu.VMEM((len(VIA_Z), nzl, p.own * nx, p.cout), BF16),
+        pltpu.VMEM((len(VIA_Z), p.own * nx, p.cout), F32),
+        pltpu.VMEM((nx, p.block, p.cout), F32),
         pltpu.VMEM((p.taps, p.rows + 2 * PAD, p.halfp), F32),
         pltpu.VMEM((p.halfp // 128, 2 * p.rows, 128), F32),
         pltpu.VMEM((2, p.rows, p.halfp), BF16),
@@ -465,22 +523,27 @@
         scratch += [dma((n,)), dma((n,))]
     vmem = pl.BlockSpec(memory_space=pltpu.VMEM)
 
+    hbm = pl.BlockSpec(memory_space=pl.ANY)
+    shapes = (
+        jax.ShapeDtypeStruct((1, pairs, p.cout), BF16),
+        jax.ShapeDtypeStruct((1, p.rows, p.cin), BF16),
+        jax.ShapeDtypeStruct((p.taps, p.own, p.cout), F32),
+        jax.ShapeDtypeStruct((p.cin,), F32),
+        jax.ShapeDtypeStruct((p.cout,), F32),
+    )
+
     def per_device(activ, gain, weight, bias, cotangent):
         outs = pl.pallas_call(
             functools.partial(kernel, p, factor),
-            out_shape=(
-                jax.ShapeDtypeStruct((1, pairs, p.cout), BF16),
-                jax.ShapeDtypeStruct((1, p.rows, p.cin), BF16),
-                jax.ShapeDtypeStruct((p.taps, p.own, p.cout), F32),
-                jax.ShapeDtypeStruct((1, p.cin), F32),
-                jax.ShapeDtypeStruct((1, p.cout), F32),
-            ),
-            in_specs=[vmem] * 5,
+            out_shape=shapes,
+            in_specs=[hbm] * 5,
             out_specs=(vmem,) * 5,
             scratch_shapes=scratch,
             compiler_params=pltpu.CompilerParams(collective_id=0, has_side_effects=True),
-        )(activ, gain.reshape(1, -1), weight, bias.reshape(1, -1), cotangent)
-        return (*outs[:3], outs[3].reshape(-1), outs[4].reshape(-1))
+        )(activ, gain, weight, bias, cotangent)
+        return pl.pallas_call(
+            hand_over, out_shape=shapes, in_specs=[vmem] * 5, out_specs=(vmem,) * 5
+        )(*outs)
 
     in_specs = (P("batch", "seq", None), P(), P(None, "seq", None), P(), P("batch", "seq", None))
     out_specs = (P("batch", "seq", None), P("batch", "seq", None), P(None, "seq", None), P(), P())

time: 63.4 us -> 54.1 us (0.85)
  local copies, waits for them, and re-layouts: 4.89 us -> 0 us
  Pallas kernels: 55.5 us -> 52.5 us
  other arithmetic: 1.31 us -> 0 us
    unnamed x10 -> x0, local copies, waits for them, and re-layouts: 3.65 us -> none
    pallas_call x1 -> x2, Pallas kernels: 55.5 us -> 52.5 us  [the longest x1 50.8 us: per_device(): pl.pallas_call(functools.partial(kernel, p, factor), out_shape=shapes, in...]
    pallas_call x1 -> x0, other arithmetic: 1.31 us -> none  [per_device(): pl.pallas_call(functools.partial(kernel, p, factor), out_shape=(jax.Shape...]
    reshape x1 -> x0, local copies, waits for them, and re-layouts: 1.25 us -> none  [per_device(): gain.reshape(1, -1)]
where the time goes in v3:
time: 54.1 us; the launch traced here: 53.1 us
  Pallas kernels  52.5 us (97%)
  between operations  0.64 us (1%)
    pallas_call x1, Pallas kernels, per_device(): pl.pallas_call(functools.partial(kernel, p, factor), out_shape=shapes, in...  50.8 us
    pallas_call x1, Pallas kernels, per_device(): pl.pallas_call(hand_over, out_shape=shapes, in_specs=[vmem] * 5, out_spec...  1.68 us

profile of v3, /device:TPU:1, one launch (start us, length us, event | category | flops | bytes accessed | tf_op | source)
XLA Modules:
  0.0 53.1 jit_solution(1712518252029736676)
XLA Ops:
  0.6 50.8 %shard_map.92 = (bf16[1,64,448]{2,1,0:T(8,128)(2,1)}, bf16[1,128,384]{2,1,0:T(8,128)(2,1)}, f32[5,6,448]{2,1,0:T(8,128)}, f32[384]{0:T(512)}, f32[448]{0:T(512)}) custom-call(bf16[1,128,384]{2,1,0:T(8,128)(2,1)} %activ_h.1, f32[384]{0:T(512)} %gain_h.1, bf16[5,6,448]{2,1,0:T(8,128)(2,1)} %weight_h.1, f32[448]{0:T(512)} %bias_h.1, bf16[1,64,448]{2,1,0:T(8,128)(2,1)} %cot_h_.1), custom_call_target="tpu_custom_call" | custom-call | tf_op jit(solution)/shard_map/pallas_call | solution.py:536
  51.4 1.7 %shard_map.93 = (bf16[1,64,448]{2,1,0:T(8,128)(2,1)}, bf16[1,128,384]{2,1,0:T(8,128)(2,1)}, f32[5,6,448]{2,1,0:T(8,128)}, f32[384]{0:T(512)}, f32[448]{0:T(512)}) custom-call(bf16[1,64,448]{2,1,0:T(8,128)(2,1)} %get-tuple-element.10.refs_0_, bf16[1,128,384]{2,1,0:T(8,128)(2,1)} %get-tuple-element.11.refs_1_, f32[5,6,448]{2,1,0:T(8,128)} %get-tuple-element.12.refs_2_, ...), custom_call_target="tpu_custom_call" | custom-call | tf_op jit(solution)/shard_map/pallas_call | solution.py:544

commit v4 on v3

--- a/solution.py
+++ b/solution.py
@@ -78,23 +78,24 @@
 TN = ((0,), (0,))
 
 
-TAPS = (2, 1, 3, 0, 4)
-GROUPS = ((0, 24, (2, 1, 3, 0)), (24, 8, (4,)))
+TAPS = (2, 1, 3, 0)
+X_FIRST = 4
+GROUPS = ((0, 24, (2, 1, 3, 4)), (24, 8, (0,)))
 VIA_Z = (3, 4)
 ORDER = (
-    ("xf", 0), ("xf", 1), ("wz", 0), ("wz", 1), ("wz", 2), ("ys", 0), ("ys", 1), ("cv", 0), ("ys", 2), ("cv", 1),
-    ("ys", 3), ("cv", 2), ("ys", 4), ("zf", 0), ("cv", 3), ("zf", 1), ("cv", 4),
+    ("xf", 0), ("xf", 1), ("wz", 0), ("wz", 1), ("wz", 2), ("ys", 0), ("ys", 1), ("x1", 0), ("cv", 0), ("ys", 2),
+    ("cv", 1), ("ys", 3), ("cv", 2), ("zf", 0), ("cv", 3), ("xs", 0), ("zf", 1), ("cv", 4),
 )
-LATE = (0, 1)
+LATE = (1,)
 
 
 def kernel(
     plan, factor,
     activ_h, gain_h, weight_h, bias_h, cot_h_,
     pooled, grad_input, grad_weight, grad_gain, grad_bias,
-    activ, gain, weight, bias, cot, s_in, act_p, cot_p, act_h, cot_h, sel, af, gf, ct, zb, wf, wx, dws, dwo, yr, xs, xo, xr, zo, zs0, zs1, zr0, zr1, ya, xb, xp, zx, wg, wh,
-    cks, io, gi_s, gi_r, pf_s, pf_r, gx, gt, gs, gz,
-    s_loc, r_loc, s_az, r_az, s_ax, r_ax, s_y, r_y, s_x, r_x, s_z, r_z, s_ya, r_ya, s_gx, r_gx, s_gz, r_gz, s_xf, r_xf, s_zf, r_zf,
+    activ, gain, weight, bias, cot, s_in, far_sem, act_p, cot_p, act_h, cot_h, sel, af, gf, ct, zb, wf, wx, dws, dwo, yr, xs, xo, xr, zo, zs0, zs1, zr0, zr1, ya, xb, xp, zx, wg, wh,
+    cks, io, gi_s, gi_r, pf_s, pf_r, gx, gt, gs, gz, bt, bx, bs, bz, fo, fs, fr, go, gb, gr,
+    s_loc, r_loc, s_az, r_az, s_ax, r_ax, s_y, r_y, s_x, r_x, s_z, r_z, s_ya, r_ya, s_gx, r_gx, s_gz, r_gz, s_xf, r_xf, s_zf, r_zf, s_bx, r_bx, s_bz, r_bz, s_f, r_f, s_g, r_g,
 ):
     p = plan
     nx, ny, nz, nzl = p.nx, p.ny, p.nz, p.nzl
@@ -132,12 +133,19 @@
     def chip_core(c, cc):
         return device(c // nx, c % nx, cc, y)
 
+    XFAR = sorted(range(1, nx), key=lambda d: -min(d, nx - d))
+    YFAR = sorted(range(1, ny), key=lambda d: -min(d, ny - d))
+    ZFAR = sorted(range(1, nz), key=lambda d: -min(d, nz - d))
+    SQUARE = sorted(
+        ((dy, dx) for dy in range(ny) for dx in range(nx)), key=lambda v: -min(v[0], ny - v[0]) - min(v[1], nx - v[1])
+    )
     barrier = pltpu.get_barrier_semaphore()
     peers = [partner]
     peers += [device(z, at_x(d), cc, y) for d in range(1, nx) for cc in (core, other)]
     peers += [device(z, x, core, at_y(d)) for d in range(1, ny)]
     far = nzl // 2
-    peers += [device(at_z(s * o), x, core, y) for o in range(1, far + 1) for s in (1, -1)]
+    near = min(2, far)
+    peers += [device(at_z(s * o), x, core, y) for o in range(1, near + 1) for s in (1, -1)]
     peers += [chip_core(c, cc) for c in (nxt, prv) for cc in (0, 1)]
     for peer in peers:
         pl.semaphore_signal(barrier, inc=1, device_id=peer, device_id_type=MESH)
@@ -173,6 +181,9 @@
 
     pl.semaphore_wait(barrier, len(peers))
 
+    for s in (1, -1):
+        pl.semaphore_signal(far_sem, inc=1, device_id=device(at_z(s * near), x, core, y), device_id_type=MESH)
+
     started = []
 
     def send(src, dst, s, r_, to):
@@ -182,6 +193,19 @@
         copy.start()
         started.append(copy)
         return copy
+
+    def share(src, dst, s, r_, to):
+        pltpu.make_async_remote_copy(
+            src_ref=src, dst_ref=dst, send_sem=s, recv_sem=r_, device_id=to, device_id_type=MESH
+        ).start()
+
+    def whole(region, sem):
+        return pltpu.make_async_remote_copy(
+            src_ref=region, dst_ref=region, send_sem=sem, recv_sem=sem, device_id=partner, device_id_type=MESH
+        )
+
+    def arrived(region, sem):
+        whole(region, sem).wait_recv()
 
     c_act = send(activ.at[0], act_p, s_loc.at[0], r_loc.at[0], partner)
     c_cot = send(cot.at[0], cot_p, s_loc.at[1], r_loc.at[1], partner)
@@ -197,16 +221,20 @@
         halos.append(send(cot.at[0, c_edge], cot_h.at[side], s_loc.at[4 + i], r_loc.at[4 + side], to))
     n_off = len(p.offsets)
     c_az = []
-    c_xf = []
     for n, k in enumerate(VIA_Z):
-        for d in range(1, nx):
-            j = (nx - 1) * n + d - 1
-            c_xf.append(send(weight.at[k], xb.at[n, x], s_xf.at[j], r_xf.at[j], device(z, at_x(d), core, y)))
+        for d in XFAR:
+            share(weight.at[k], xb.at[n, x], s_xf.at[0], r_xf.at[n], device(z, at_x(d), core, y))
         xb[n, x] = weight[k]
-    for k in range(taps - len(VIA_Z)):
-        for i, o in enumerate(p.offsets):
-            j = k * n_off + i
-            c_az.append(send(weight.at[k], zb.at[z_lo, k], s_az.at[j], r_az.at[j], device(at_z(sign * o), x, core, y)))
+    direct = range(taps - len(VIA_Z))
+
+    def weights_out(wanted):
+        for k in direct:
+            for o in sorted(p.offsets, key=lambda v: -abs(v)):
+                if (abs(o) <= near) == wanted:
+                    to = device(at_z(sign * o), x, core, y)
+                    share(weight.at[k], zb.at[z_lo, k], s_az.at[0], r_az.at[k], to)
+
+    weights_out(True)
     zb[z_lo] = weight[...]
 
     def activate(start, count):
@@ -222,26 +250,43 @@
     def cot_shift(d):
         return ct[PAD + d:PAD + d + rows, :].astype(BF16)
 
-    c_y = [None] * taps
-
     def y_send(k, part):
         for t in range(ny):
             dwo[t, k] = part[:, 128 * t:128 * t + 128]
             dws[t, k] = part[:, 128 * t:128 * t + 128].astype(BF16)
-        c_y[k] = []
-        for d in range(1, ny):
-            i = (ny - 1) * k + d - 1
-            c_y[k].append(send(dws.at[at_y(d), k], yr.at[d - 1, k], s_y.at[i], r_y.at[i], device(z, x, core, at_y(d))))
+        for d in YFAR:
+            share(dws.at[at_y(d), k], yr.at[k, d - 1], s_y.at[0], r_y.at[k], device(z, x, core, at_y(d)))
 
     c_act.wait_recv()
     put(pl.multiple_of(PAD + rows * other, 8), dot(act_p[...], mine, NN))
     c_cot.wait_recv()
     ct[pl.ds(pl.multiple_of(PAD + pairs * other, 8), pairs), 0:p.cout] = cot_p[...].astype(F32)
+    bias_part = jnp.sum(ct[PAD:PAD + rows, :], axis=0, keepdims=True)
+    for t in range(ny):
+        bt[t:t + 1, :] = bias_part[:, 128 * t:128 * t + 128]
+
+    def bias_out():
+        for dy, dx in SQUARE:
+            i = dy * nx + dx - 1
+            if i >= 0:
+                share(bt, bx.at[i], s_bx.at[0], r_bx.at[0], device(z, at_x(dx), core, at_y(dy)))
+
+    def bias_sum(_):
+        arrived(bx, r_bx.at[0])
+        total = bt[...]
+        for i in range(nx * ny - 1):
+            total = total + bx[i]
+        bs[...] = total
+        for d in ZFAR:
+            share(bs, bz.at[d - 1], s_bz.at[0], r_bz.at[0], device(at_z(d), x, core, y))
+
     activate(PAD, 2 * rows)
     even, odd = strided(gf, PAD).astype(BF16), strided(gf, PAD + 1).astype(BF16)
     here = cot_shift(0)
     e0, o0 = dot(even, here, TN)[0:half], dot(odd, here, TN)[0:half]
     y_send(2, 0.5 * (e0 + o0))
+    pl.semaphore_wait(far_sem, 2)
+    weights_out(False)
 
     for s in (0, 1):
         for src, dst, i in ((activ.at[0, a_edge], act_h, 2), (cot.at[0, c_edge], cot_h, 4)):
@@ -255,45 +300,41 @@
     ct[0:PAD, 0:p.cout] = (cot_h[1].astype(F32) * before)[edge - PAD:edge]
     ct[PAD + rows:, 0:p.cout] = (cot_h[0].astype(F32) * after)[0:PAD]
     up, down = cot_shift(1), cot_shift(-1)
+    e_down = dot(even, down, TN)[0:half]
+    part = 0.5 * (e_down + dot(odd, down, TN)[0:half])
+    for xx in range(nx):
+        fo[xx] = part[block * xx:block * (xx + 1)]
+        fs[xx] = part[block * xx:block * (xx + 1)].astype(BF16)
+    for d in XFAR:
+        share(fs.at[at_x(d)], fr.at[d - 1], s_f.at[0], r_f.at[0], device(z, at_x(d), core, y))
     o_up = dot(odd, up, TN)[0:half]
     y_send(1, 0.5 * (e0 + o_up))
-    e_down = dot(even, down, TN)[0:half]
     y_send(3, 0.5 * (e_down + o0))
     y_send(0, 0.5 * (dot(even, up, TN)[0:half] + o_up))
-    y_send(4, 0.5 * (e_down + dot(odd, down, TN)[0:half]))
     put(0, (dot(act_h[1], mine, NN) * before)[edge - PAD:edge])
     put(PAD + 2 * rows, (dot(act_h[0], mine, NN) * after)[0:PAD])
     activate(0, PAD)
     activate(PAD + 2 * rows, PAD)
 
-    c_ax = []
-
     def weights_z(k):
-        for c in c_az[n_off * k:n_off * (k + 1)]:
-            c.wait_recv()
+        arrived(zb.at[pl.ds(0, n_off), k], r_az.at[k])
         for zz in range(nzl):
             wf[k % 2, own * zz:own * (zz + 1)] = zb[zz, k].astype(F32)
         wx[x, k] = wf[k % 2].astype(BF16)
-        for d in range(1, nx):
-            i = (nx - 1) * k + d - 1
-            c_ax.append(send(wx.at[x, k], wx.at[x, k], s_ax.at[i], r_ax.at[i], device(z, at_x(d), core, y)))
-
-    c_zf = []
+        for d in XFAR:
+            share(wx.at[x, k], wx.at[x, k], s_ax.at[0], r_ax.at[k], device(z, at_x(d), core, y))
 
     def weights_x(n):
-        for c in c_xf[(nx - 1) * n:(nx - 1) * (n + 1)]:
-            c.wait_recv()
+        arrived(xb.at[n, pl.ds(0, nx - 1)], r_xf.at[n])
         for xx in range(nx):
             wg[n, own * xx:own * (xx + 1)] = xb[n, xx].astype(F32)
         xp[n] = wg[n].astype(BF16)
-        for i, o in enumerate(p.offsets):
-            j = n * n_off + i
-            c_zf.append(send(xp.at[n], zx.at[n, z_lo], s_zf.at[j], r_zf.at[j], device(at_z(sign * o), x, core, y)))
+        for o in sorted(p.offsets, key=lambda v: -abs(v)):
+            share(xp.at[n], zx.at[n, z_lo], s_zf.at[0], r_zf.at[n], device(at_z(sign * o), x, core, y))
         zx[n, z_lo] = xp[n]
 
     def weights_last(n):
-        for c in c_zf[n_off * n:n_off * (n + 1)]:
-            c.wait_recv()
+        arrived(zx.at[n, pl.ds(0, n_off)], r_zf.at[n])
         for zz in range(nzl):
             rows_z = zx[n, zz].astype(F32)
             for xx in range(nx):
@@ -301,44 +342,49 @@
         for xx in range(nx):
             wx[xx, VIA_Z[n]] = wh[xx].astype(BF16)
 
-    c_x = {}
-
     def y_sum(n):
         k = TAPS[n]
-        for c in c_y[k]:
-            c.wait_recv()
+        arrived(yr.at[k], r_y.at[k])
+        if n == 0:
+            bias_out()
         total = dwo[y, k]
         for d in range(ny - 1):
-            total = total + yr[d, k].astype(F32)
+            total = total + yr[k, d].astype(F32)
         for xx in range(nx):
             piece = total[block * xx:block * (xx + 1)]
             xo[xx, k] = piece
             xs[xx, k] = piece.astype(BF16)
-        c_x[k] = []
-        for d in range(1, nx):
-            i = (nx - 1) * k + d - 1
-            c_x[k].append(send(xs.at[at_x(d), k], xr.at[d - 1, k], s_x.at[i], r_x.at[i], device(z, at_x(d), core, y)))
+        for d in XFAR:
+            share(xs.at[at_x(d), k], xr.at[k, d - 1], s_x.at[0], r_x.at[k], device(z, at_x(d), core, y))
+
+    def x_first(_):
+        arrived(fr, r_f.at[0])
+        total = fo[x]
+        for d in range(nx - 1):
+            total = total + fr[d].astype(F32)
+        for t in range(ny):
+            go[t] = total[:, 128 * t:128 * t + 128]
+            gb[t] = total[:, 128 * t:128 * t + 128].astype(BF16)
+        for d in YFAR:
+            share(gb.at[at_y(d)], gr.at[d - 1], s_g.at[0], r_g.at[0], device(z, x, core, at_y(d)))
 
     z_s, z_r = (zs0, zs1), (zr0, zr1)
-    c_z = []
-
     def x_sum(g):
         base, length, members = GROUPS[g]
         zo[:, base:base + length, :] = jnp.zeros((nzl, length, 128), F32)
         for n, k in enumerate(members):
-            for c in c_x[k]:
-                c.wait_recv()
-            total = xo[x, k]
-            for d in range(nx - 1):
-                total = total + xr[d, k].astype(F32)
+            if k == X_FIRST:
+                arrived(gr, r_g.at[0])
+            else:
+                arrived(xr.at[k], r_x.at[k])
+            total = go[y] if k == X_FIRST else xo[x, k]
+            for d in range((ny if k == X_FIRST else nx) - 1):
+                total = total + (gr[d] if k == X_FIRST else xr[k, d]).astype(F32)
             for zz in range(nzl):
                 zo[zz, base + own * n:base + own * (n + 1), :] = total[own * zz:own * (zz + 1)]
         z_s[g][...] = zo[:, base:base + length, :].astype(BF16)
-        for d in range(1, nz):
-            i = (nz - 1) * g + d - 1
-            c_z.append(
-                send(z_s[g].at[at_z(d) % nzl], z_r[g].at[d - 1], s_z.at[i], r_z.at[i], device(at_z(d), x, core, y))
-            )
+        for d in ZFAR:
+            share(z_s[g].at[at_z(d) % nzl], z_r[g].at[d - 1], s_z.at[g], r_z.at[g], device(at_z(d), x, core, y))
 
     acc = [None]
     cot_all = ct[:, 0:p.cout].astype(BF16)
@@ -346,8 +392,7 @@
 
     def convs(k):
         if k not in VIA_Z:
-            for c in c_ax[(nx - 1) * k:(nx - 1) * (k + 1)]:
-                c.wait_recv()
+            arrived(wx.at[pl.ds(0, nx - 1), k], r_ax.at[k])
         w = wx[:, k].reshape(half, p.cout)
         add = dot(shifted[k], w, NN) + dot(shifted[k + 1], w, NN)
         acc[0] = add if acc[0] is None else acc[0] + add
@@ -356,7 +401,7 @@
             cks[k, :, half:] = jnp.zeros((rows + 2 * PAD, p.halfp - half), F32)
 
     for step, k in ORDER:
-        {"wz": weights_z, "ys": y_sum, "cv": convs, "xs": x_sum, "xf": weights_x, "zf": weights_last}[step](k)
+        {"wz": weights_z, "ys": y_sum, "cv": convs, "xs": x_sum, "xf": weights_x, "zf": weights_last, "x1": x_first}[step](k)
     conv = acc[0]
     conv = 0.5 * conv
     for h in (0, 1):
@@ -385,26 +430,21 @@
         ).astype(BF16)
     c_gi = send(gi_s.at[other], gi_r, s_loc.at[7], r_loc.at[7], partner)
 
-    gt[...] = jnp.zeros_like(gt)
     for t in range(tiles):
         gt[0, t:t + 1, :] = gain_part[:, 128 * t:128 * t + 128]
-    bias_part = jnp.sum(ct[pl.ds(pl.multiple_of(PAD + pairs * core, 8), pairs), :], axis=0, keepdims=True)
-    for t in range(ny):
-        gt[0, 4 + t:5 + t, :] = bias_part[:, 128 * t:128 * t + 128]
-    c_gx = []
-    for flip in (0, 1):
-        for dy in range(ny):
-            for dx in range(nx):
-                i = (flip * ny + dy) * nx + dx
-                if i > 0:
-                    cc = core if flip == 0 else other
-                    c_gx.append(send(gt.at[0], gx.at[i], s_gx.at[i], r_gx.at[i], device(z, at_x(dx), cc, at_y(dy))))
+    for dy, dx in SQUARE:
+        for flip in (0, 1):
+            i = (flip * ny + dy) * nx + dx
+            if i > 0:
+                cc = core if flip == 0 else other
+                share(gt.at[0], gx.at[i], s_gx.at[0], r_gx.at[0], device(z, at_x(dx), cc, at_y(dy)))
 
     for g in LATE:
         x_sum(g)
-
-    for c in c_gx:
-        c.wait_recv()
+    bias_sum(0)
+
+    others = gx.at[pl.ds(1, 2 * nx * ny - 1)]
+    arrived(others, r_gx.at[0])
     same = gt[0]
     for i in range(1, ny * nx):
         same = same + gx[i]
@@ -413,20 +453,18 @@
         flipped = flipped + gx[ny * nx + i]
     first = jnp.where(core == 0, same, flipped)
     second = jnp.where(core == 0, flipped, same)
-    gs[0:2, :] = first[0:2]
-    gs[2:4, :] = second[0:2]
-    gs[4:8, :] = (first + second)[4:8]
-    c_gz = []
-    for d in range(1, nz):
-        c_gz.append(send(gs, gz.at[d - 1], s_gz.at[d - 1], r_gz.at[d - 1], device(at_z(d), x, core, y)))
+    gs[0:tiles, :] = first
+    gs[tiles:2 * tiles, :] = second
+    for d in ZFAR:
+        share(gs, gz.at[d - 1], s_gz.at[0], r_gz.at[0], device(at_z(d), x, core, y))
 
     c_pf.wait_recv()
     pooled[0] = (pf_s[core] + pf_r[...] + bias[...].reshape(1, p.cout)).astype(BF16)
     c_gi.wait_recv()
     grad_input[0] = (dot(gi_s[core], mine, NT) + dot(gi_r[...], sel[other], NT)).astype(BF16)
 
-    for c in c_z:
-        c.wait_recv()
+    for g in range(len(GROUPS)):
+        arrived(z_r[g], r_z.at[g])
     for g, (base, length, members) in enumerate(GROUPS):
         final = zo[z_lo, base:base + length, :]
         for d in range(nz - 1):
@@ -436,17 +474,22 @@
     for d in range(1, ny):
         c_ya.append(send(ya.at[y], ya.at[y], s_ya.at[d - 1], r_ya.at[d - 1], device(z, x, core, at_y(d))))
 
-    for c in c_gz:
-        c.wait_recv()
+    arrived(gz, r_gz.at[0])
     total = gs[...]
     for d in range(nz - 1):
         total = total + gz[d]
     total = total * factor
     halves = [
-        jnp.concatenate([total[2 * h + t:2 * h + t + 1] for t in range(tiles)], axis=1) for h in (0, 1)
+        jnp.concatenate([total[tiles * h + t:tiles * h + t + 1] for t in range(tiles)], axis=1) for h in (0, 1)
     ]
     grad_gain[...] = (picked(halves[0], sel[0], NT) + picked(halves[1], sel[1], NT)).reshape(p.cin)
-    grad_bias[...] = jnp.concatenate([total[4 + t:5 + t] for t in range(ny)], axis=1)[:, 0:p.cout].reshape(p.cout)
+
+    arrived(bz, r_bz.at[0])
+    total = bs[...]
+    for d in range(nz - 1):
+        total = total + bz[d]
+    total = total * factor
+    grad_bias[...] = jnp.concatenate([total[t:t + 1] for t in range(ny)], axis=1)[:, 0:p.cout].reshape(p.cout)
 
     for c in c_ya:
         c.wait_recv()
@@ -457,6 +500,15 @@
             grad_weight[k] = wide[:, 0:p.cout]
     for c in started:
         c.wait_send()
+    n_direct, n_via, n_y = len(direct), len(VIA_Z), len(TAPS)
+    for region, sem in (
+        (xb.at[:, pl.ds(0, nx - 1)], s_xf), (zb.at[pl.ds(0, n_off), pl.ds(0, n_direct)], s_az), (yr, s_y), (bx, s_bx),
+        (bz, s_bz), (fr, s_f), (gr, s_g), (wx.at[pl.ds(0, nx - 1), pl.ds(0, n_direct)], s_ax),
+        (zx.at[:, pl.ds(0, n_off)], s_zf), (xr, s_x), (others, s_gx), (gz, s_gz),
+    ):
+        whole(region, sem.at[0]).wait_send()
+    for g in range(len(GROUPS)):
+        whole(z_r[g], s_z.at[g]).wait_send()
 
 
 def hand_over(*refs):
@@ -470,10 +522,10 @@
     pairs = p.rows // 2
     zrows = sum(length for _, length, _ in GROUPS)
     dma = pltpu.SemaphoreType.DMA
+    n_direct, n_via, n_y = p.taps - len(VIA_Z), len(VIA_Z), len(TAPS)
     sems = (
-        8, p.taps * len(p.offsets), p.taps * (nx - 1), p.taps * (ny - 1), p.taps * (nx - 1),
-        len(GROUPS) * (nz - 1), ny - 1, 2 * nx * ny, nz - 1,
-        len(VIA_Z) * (nx - 1), len(VIA_Z) * len(p.offsets),
+        (8, 8), (1, n_direct), (1, n_direct), (1, n_y), (1, n_y), (len(GROUPS),) * 2, (ny - 1, ny - 1),
+        (1, 1), (1, 1), (1, n_via), (1, n_via), (1, 1), (1, 1), (1, 1), (1, 1),
     )
     scratch = [
         pltpu.VMEM((1, p.rows, p.cin), BF16),
@@ -482,6 +534,7 @@
         pltpu.VMEM((p.cout,), F32),
         pltpu.VMEM((1, pairs, p.cout), BF16),
         dma((5,)),
+        pltpu.SemaphoreType.REGULAR,
         pltpu.VMEM((p.rows, p.cin), BF16),
         pltpu.VMEM((pairs, p.cout), BF16),
         pltpu.VMEM((2, 16, p.cin), BF16),
@@ -495,10 +548,10 @@
         pltpu.VMEM((nx, p.taps, p.block, p.cout), BF16),
         pltpu.VMEM((ny, p.taps, p.half, 128), BF16),
         pltpu.VMEM((ny, p.taps, p.half, 128), F32),
-        pltpu.VMEM((ny - 1, p.taps, p.half, 128), BF16),
+        pltpu.VMEM((len(TAPS), ny - 1, p.half, 128), BF16),
         pltpu.VMEM((nx, p.taps, p.block, 128), BF16),
         pltpu.VMEM((nx, p.taps, p.block, 128), F32),
-        pltpu.VMEM((nx - 1, p.taps, p.block, 128), BF16),
+        pltpu.VMEM((len(TAPS), nx - 1, p.block, 128), BF16),
         pltpu.VMEM((nzl, zrows, 128), F32),
         *[pltpu.VMEM((nzl, length, 128), BF16) for _, length, _ in GROUPS],
         *[pltpu.VMEM((nz - 1, length, 128), BF16) for _, length, _ in GROUPS],
@@ -514,16 +567,26 @@
         pltpu.VMEM((p.rows, p.halfp), BF16),
         pltpu.VMEM((2, pairs, p.cout), F32),
         pltpu.VMEM((pairs, p.cout), F32),
-        pltpu.VMEM((2 * nx * ny, 8, 128), F32),
-        pltpu.VMEM((1, 8, 128), F32),
-        pltpu.VMEM((8, 128), F32),
-        pltpu.VMEM((nz - 1, 8, 128), F32),
+        pltpu.VMEM((2 * nx * ny, p.halfp // 128, 128), F32),
+        pltpu.VMEM((1, p.halfp // 128, 128), F32),
+        pltpu.VMEM((p.halfp // 64, 128), F32),
+        pltpu.VMEM((nz - 1, p.halfp // 64, 128), F32),
+        pltpu.VMEM((ny, 128), F32),
+        pltpu.VMEM((nx * ny - 1, ny, 128), F32),
+        pltpu.VMEM((ny, 128), F32),
+        pltpu.VMEM((nz - 1, ny, 128), F32),
+        pltpu.VMEM((nx, p.block, p.coutp), F32),
+        pltpu.VMEM((nx, p.block, p.coutp), BF16),
+        pltpu.VMEM((nx - 1, p.block, p.coutp), BF16),
+        pltpu.VMEM((ny, p.block, 128), F32),
+        pltpu.VMEM((ny, p.block, 128), BF16),
+        pltpu.VMEM((ny - 1, p.block, 128), BF16),
     ]
-    for n in sems:
-        scratch += [dma((n,)), dma((n,))]
+    for sent, received in sems:
+        scratch += [dma((sent,)), dma((received,))]
     vmem = pl.BlockSpec(memory_space=pltpu.VMEM)
 
-    hbm = pl.BlockSpec(memory_space=pl.ANY)
+    hbm = pl.BlockSpec(memory_space=pltpu.HBM)
     shapes = (
         jax.ShapeDtypeStruct((1, pairs, p.cout), BF16),
         jax.ShapeDtypeStruct((1, p.rows, p.cin), BF16),
@@ -542,7 +605,7 @@
             compiler_params=pltpu.CompilerParams(collective_id=0, has_side_effects=True),
         )(activ, gain, weight, bias, cotangent)
         return pl.pallas_call(
-            hand_over, out_shape=shapes, in_specs=[vmem] * 5, out_specs=(vmem,) * 5
+            hand_over, out_shape=shapes, in_specs=[vmem] * 5, out_specs=(vmem,) * 5,
         )(*outs)
 
     in_specs = (P("batch", "seq", None), P(), P(None, "seq", None), P(), P("batch", "seq", None))

time: 54.1 us -> 50.1 us (0.926); the launches traced: 53.1 us -> 49.9 us
  Pallas kernels: 52.5 us -> 49.3 us
    pallas_call x1, Pallas kernels: 50.8 us -> 47.6 us  [per_device(): pl.pallas_call(functools.partial(kernel, p, factor), out_shape=shapes, in...]
where the time goes in v4:
time: 50.1 us; the launch traced here: 49.9 us
  Pallas kernels  49.3 us (98%)
  between operations  0.64 us (1%)
    pallas_call x1, Pallas kernels, per_device(): pl.pallas_call(functools.partial(kernel, p, factor), out_shape=shapes, in...  47.6 us
    pallas_call x1, Pallas kernels, per_device(): pl.pallas_call(hand_over, out_shape=shapes, in_specs=[vmem] * 5, out_spec...  1.68 us

profile of v4, /device:TPU:1, one launch (start us, length us, event | category | flops | bytes accessed | tf_op | source)
XLA Modules:
  0.0 49.9 jit_solution(7046130531980469712)
XLA Ops:
  0.6 47.6 %shard_map.92 = (bf16[1,64,448]{2,1,0:T(8,128)(2,1)}, bf16[1,128,384]{2,1,0:T(8,128)(2,1)}, f32[5,6,448]{2,1,0:T(8,128)}, f32[384]{0:T(512)}, f32[448]{0:T(512)}) custom-call(bf16[1,128,384]{2,1,0:T(8,128)(2,1)} %activ_h.1, f32[384]{0:T(512)} %gain_h.1, bf16[5,6,448]{2,1,0:T(8,128)(2,1)} %weight_h.1, f32[448]{0:T(512)} %bias_h.1, bf16[1,64,448]{2,1,0:T(8,128)(2,1)} %cot_h_.1), custom_call_target="tpu_custom_call" | custom-call | tf_op jit(solution)/shard_map/pallas_call | solution.py:599
  48.2 1.7 %shard_map.93 = (bf16[1,64,448]{2,1,0:T(8,128)(2,1)}, bf16[1,128,384]{2,1,0:T(8,128)(2,1)}, f32[5,6,448]{2,1,0:T(8,128)}, f32[384]{0:T(512)}, f32[448]{0:T(512)}) custom-call(bf16[1,64,448]{2,1,0:T(8,128)(2,1)} %get-tuple-element.10.refs_0_, bf16[1,128,384]{2,1,0:T(8,128)(2,1)} %get-tuple-element.11.refs_1_, f32[5,6,448]{2,1,0:T(8,128)} %get-tuple-element.12.refs_2_, ...), custom_call_target="tpu_custom_call" | custom-call | tf_op jit(solution)/shard_map/pallas_call | solution.py:607

commit v5 on v4

--- a/solution.py
+++ b/solution.py
@@ -83,7 +83,7 @@
 GROUPS = ((0, 24, (2, 1, 3, 4)), (24, 8, (0,)))
 VIA_Z = (3, 4)
 ORDER = (
-    ("xf", 0), ("xf", 1), ("wz", 0), ("wz", 1), ("wz", 2), ("ys", 0), ("ys", 1), ("x1", 0), ("cv", 0), ("ys", 2),
+    ("xf", 0), ("xf", 1), ("bx", 0), ("wz", 0), ("wz", 1), ("wz", 2), ("bs", 0), ("ys", 0), ("ys", 1), ("x1", 0), ("cv", 0), ("ys", 2),
     ("cv", 1), ("ys", 3), ("cv", 2), ("zf", 0), ("cv", 3), ("xs", 0), ("zf", 1), ("cv", 4),
 )
 LATE = (1,)
@@ -94,7 +94,7 @@
     activ_h, gain_h, weight_h, bias_h, cot_h_,
     pooled, grad_input, grad_weight, grad_gain, grad_bias,
     activ, gain, weight, bias, cot, s_in, far_sem, act_p, cot_p, act_h, cot_h, sel, af, gf, ct, zb, wf, wx, dws, dwo, yr, xs, xo, xr, zo, zs0, zs1, zr0, zr1, ya, xb, xp, zx, wg, wh,
-    cks, io, gi_s, gi_r, pf_s, pf_r, gx, gt, gs, gz, bt, bx, bs, bz, fo, fs, fr, go, gb, gr,
+    cks, io, gi_s, gi_r, pf_s, pf_r, gx, gt, gs, gz, bt, bu, bx, bs, bz, fo, fs, fr, go, gb, gr,
     s_loc, r_loc, s_az, r_az, s_ax, r_ax, s_y, r_y, s_x, r_x, s_z, r_z, s_ya, r_ya, s_gx, r_gx, s_gz, r_gz, s_xf, r_xf, s_zf, r_zf, s_bx, r_bx, s_bz, r_bz, s_f, r_f, s_g, r_g,
 ):
     p = plan
@@ -265,17 +265,23 @@
     for t in range(ny):
         bt[t:t + 1, :] = bias_part[:, 128 * t:128 * t + 128]
 
-    def bias_out():
-        for dy, dx in SQUARE:
-            i = dy * nx + dx - 1
-            if i >= 0:
-                share(bt, bx.at[i], s_bx.at[0], r_bx.at[0], device(z, at_x(dx), core, at_y(dy)))
+    for d in YFAR:
+        share(bt, bx.at[d - 1], s_bx.at[0], r_bx.at[0], device(z, x, core, at_y(d)))
+
+    def bias_x(_):
+        arrived(bx.at[pl.ds(0, ny - 1)], r_bx.at[0])
+        total = bt[...]
+        for i in range(ny - 1):
+            total = total + bx[i]
+        bu[...] = total
+        for d in XFAR:
+            share(bu, bx.at[ny - 2 + d], s_bx.at[1], r_bx.at[1], device(z, at_x(d), core, y))
 
     def bias_sum(_):
-        arrived(bx, r_bx.at[0])
-        total = bt[...]
-        for i in range(nx * ny - 1):
-            total = total + bx[i]
+        arrived(bx.at[pl.ds(ny - 1, nx - 1)], r_bx.at[1])
+        total = bu[...]
+        for i in range(nx - 1):
+            total = total + bx[ny - 1 + i]
         bs[...] = total
         for d in ZFAR:
             share(bs, bz.at[d - 1], s_bz.at[0], r_bz.at[0], device(at_z(d), x, core, y))
@@ -345,8 +351,6 @@
     def y_sum(n):
         k = TAPS[n]
         arrived(yr.at[k], r_y.at[k])
-        if n == 0:
-            bias_out()
         total = dwo[y, k]
         for d in range(ny - 1):
             total = total + yr[k, d].astype(F32)
@@ -401,7 +405,7 @@
             cks[k, :, half:] = jnp.zeros((rows + 2 * PAD, p.halfp - half), F32)
 
     for step, k in ORDER:
-        {"wz": weights_z, "ys": y_sum, "cv": convs, "xs": x_sum, "xf": weights_x, "zf": weights_last, "x1": x_first}[step](k)
+        {"wz": weights_z, "ys": y_sum, "cv": convs, "xs": x_sum, "xf": weights_x, "zf": weights_last, "x1": x_first, "bx": bias_x, "bs": bias_sum}[step](k)
     conv = acc[0]
     conv = 0.5 * conv
     for h in (0, 1):
@@ -441,7 +445,6 @@
 
     for g in LATE:
         x_sum(g)
-    bias_sum(0)
 
     others = gx.at[pl.ds(1, 2 * nx * ny - 1)]
     arrived(others, r_gx.at[0])
@@ -502,13 +505,15 @@
         c.wait_send()
     n_direct, n_via, n_y = len(direct), len(VIA_Z), len(TAPS)
     for region, sem in (
-        (xb.at[:, pl.ds(0, nx - 1)], s_xf), (zb.at[pl.ds(0, n_off), pl.ds(0, n_direct)], s_az), (yr, s_y), (bx, s_bx),
+        (xb.at[:, pl.ds(0, nx - 1)], s_xf), (zb.at[pl.ds(0, n_off), pl.ds(0, n_direct)], s_az), (yr, s_y),
         (bz, s_bz), (fr, s_f), (gr, s_g), (wx.at[pl.ds(0, nx - 1), pl.ds(0, n_direct)], s_ax),
         (zx.at[:, pl.ds(0, n_off)], s_zf), (xr, s_x), (others, s_gx), (gz, s_gz),
     ):
         whole(region, sem.at[0]).wait_send()
     for g in range(len(GROUPS)):
         whole(z_r[g], s_z.at[g]).wait_send()
+    whole(bx.at[pl.ds(0, ny - 1)], s_bx.at[0]).wait_send()
+    whole(bx.at[pl.ds(ny - 1, nx - 1)], s_bx.at[1]).wait_send()
 
 
 def hand_over(*refs):
@@ -525,7 +530,7 @@
     n_direct, n_via, n_y = p.taps - len(VIA_Z), len(VIA_Z), len(TAPS)
     sems = (
         (8, 8), (1, n_direct), (1, n_direct), (1, n_y), (1, n_y), (len(GROUPS),) * 2, (ny - 1, ny - 1),
-        (1, 1), (1, 1), (1, n_via), (1, n_via), (1, 1), (1, 1), (1, 1), (1, 1),
+        (1, 1), (1, 1), (1, n_via), (1, n_via), (2, 2), (1, 1), (1, 1), (1, 1),
     )
     scratch = [
         pltpu.VMEM((1, p.rows, p.cin), BF16),
@@ -572,7 +577,8 @@
         pltpu.VMEM((p.halfp // 64, 128), F32),
         pltpu.VMEM((nz - 1, p.halfp // 64, 128), F32),
         pltpu.VMEM((ny, 128), F32),
-        pltpu.VMEM((nx * ny - 1, ny, 128), F32),
+        pltpu.VMEM((ny, 128), F32),
+        pltpu.VMEM((ny - 1 + nx - 1, ny, 128), F32),
         pltpu.VMEM((ny, 128), F32),
         pltpu.VMEM((nz - 1, ny, 128), F32),
         pltpu.VMEM((nx, p.block, p.coutp), F32),

time: 50.1 us -> 49 us (0.978)
  Pallas kernels: 49.3 us -> 48.2 us
    pallas_call x1, Pallas kernels: 47.6 us -> 46.5 us  [per_device(): pl.pallas_call(functools.partial(kernel, p, factor), out_shape=shapes, in...]
where the time goes in v5:
time: 49 us; the launch traced here: 48.8 us
  Pallas kernels  48.2 us (98%)
  between operations  0.64 us (1%)
    pallas_call x1, Pallas kernels, per_device(): pl.pallas_call(functools.partial(kernel, p, factor), out_shape=shapes, in...  46.5 us
    pallas_call x1, Pallas kernels, per_device(): pl.pallas_call(hand_over, out_shape=shapes, in_specs=[vmem] * 5, out_spec...  1.68 us

profile of v5, /device:TPU:1, one launch (start us, length us, event | category | flops | bytes accessed | tf_op | source)
XLA Modules:
  0.0 48.8 jit_solution(8774445023715445589)
XLA Ops:
  0.6 46.5 %shard_map.92 = (bf16[1,64,448]{2,1,0:T(8,128)(2,1)}, bf16[1,128,384]{2,1,0:T(8,128)(2,1)}, f32[5,6,448]{2,1,0:T(8,128)}, f32[384]{0:T(512)}, f32[448]{0:T(512)}) custom-call(bf16[1,128,384]{2,1,0:T(8,128)(2,1)} %activ_h.1, f32[384]{0:T(512)} %gain_h.1, bf16[5,6,448]{2,1,0:T(8,128)(2,1)} %weight_h.1, f32[448]{0:T(512)} %bias_h.1, bf16[1,64,448]{2,1,0:T(8,128)(2,1)} %cot_h_.1), custom_call_target="tpu_custom_call" | custom-call | tf_op jit(solution)/shard_map/pallas_call | solution.py:605
  47.1 1.7 %shard_map.93 = (bf16[1,64,448]{2,1,0:T(8,128)(2,1)}, bf16[1,128,384]{2,1,0:T(8,128)(2,1)}, f32[5,6,448]{2,1,0:T(8,128)}, f32[384]{0:T(512)}, f32[448]{0:T(512)}) custom-call(bf16[1,64,448]{2,1,0:T(8,128)(2,1)} %get-tuple-element.10.refs_0_, bf16[1,128,384]{2,1,0:T(8,128)(2,1)} %get-tuple-element.11.refs_1_, f32[5,6,448]{2,1,0:T(8,128)} %get-tuple-element.12.refs_2_, ...), custom_call_target="tpu_custom_call" | custom-call | tf_op jit(solution)/shard_map/pallas_call | solution.py:613
